TPU v7x, 128 devices: a whole 4x4x4 slice. The times are simulated.
128 devices in a mesh: lat: 32 (over z, y, core), ch: 4 (over x).
Axes of the slice: x: 4, y: 4, z: 4, core: 2. Of those that a mesh axis runs over, the one named last changes fastest.
Arguments:
- state: float32 [1, 96, 180, 768], P(None, 'lat', None, 'ch'), may hold values from -30 to 30
- norm_gains: bfloat16 [2, 768], P(None, 'ch'), may hold values from 0.099609375 to 1.8984375
- channel_biases: bfloat16 [3, 768], P(None, 'ch'), may hold values from -2 to 2
- filter_in: float32 [2, 8, 96, 96], P(None, 'ch'), may hold values from -0.4375 to 0.4375
- filter_in_bias: float32 [2, 8, 96], P(None, 'ch'), may hold values from -2 to 2
- filter_out: float32 [2, 8, 96, 96], P(None, 'ch'), may hold values from -0.4375 to 0.4375
- filter_out_bias: float32 [2, 8, 96], P(None, 'ch'), may hold values from -2 to 2
- up_weight: bfloat16 [768, 3072], P(None, 'ch'), may hold values from -0.21875 to 0.21875
- up_bias: bfloat16 [3072], P('ch'), may hold values from -2 to 2
- down_weight: bfloat16 [3072, 768], P('ch'), may hold values from -0.109375 to 0.109375
Outputs:
- final_state: float32 [1, 96, 180, 768], P(None, 'lat', None, 'ch')
All inputs are finite; a program needn't handle non-finite values.
Results may differ from a plain program's by a relative error of at most 0.0012.
Values may be sent and summed in bfloat16 or wider, within the bound.
A program may use at most 128 MiB of HBM per device.

v0:
```python
import math

import jax
import jax.numpy as jnp
from jax import lax
from jax.sharding import PartitionSpec as P

D = 768
M = 64
STEPS = 4


EPS = 1e-05
SHRINK = 0.01
HIGH = lax.Precision.HIGHEST


def sent_to_all(shard, axis):
    length = lax.axis_size(axis)
    return lax.all_to_all(
        jnp.broadcast_to(shard[None], (length, *shard.shape)), axis, 0, 0, tiled=True
    )


def of_everyone(shard, axis):
    everything = sent_to_all(shard, axis)
    return jnp.sum(everything, axis=0)


def in_one(arrays, axis):
    ravelled, at, outs = (jnp.concatenate([a.reshape(-1) for a in arrays]), 0, [])
    total = of_everyone(ravelled, axis)
    for a in arrays:
        outs.append(total[at : at + a.size].reshape(a.shape))
        at += a.size
    return tuple(outs)


def sent_together(arrays, axis, dim, along):
    both = jnp.concatenate(arrays, axis=along)
    result, at, outs = (lax.all_gather(both, axis, axis=dim, tiled=True), 0, [])
    for a in arrays:
        outs.append(lax.slice_in_dim(result, at, at + a.shape[along], axis=along))
        at += a.shape[along]
    return tuple(outs)


def sent_together_2(arrays, axis, dim, along):
    widths = [math.prod(a.shape[along:]) for a in arrays]
    both = jnp.concatenate(
        [a.reshape(*a.shape[:along], w) for a, w in zip(arrays, widths)], axis=along
    )
    result = lax.all_gather(both, axis, axis=dim, tiled=True)
    tiles = jnp.split(result, [sum(widths[:k]) for k in range(1, len(widths))], axis=along)
    return tuple(
        (b.reshape(*result.shape[:along], *a.shape[along:]) for a, b in zip(arrays, tiles))
    )


def longitude_tables(width, modes):
    column = jnp.arange(width, dtype=jnp.int32)[:, None]
    order = jnp.arange(modes, dtype=jnp.int32)[None, :]
    angle = 2.0 * math.pi / width * (column * order % width).astype(jnp.float32)
    doubled = jnp.where(order == 0, 1.0, 2.0).astype(jnp.float32)
    return (jnp.cos(angle), jnp.sin(angle), jnp.cos(angle) * doubled, jnp.sin(angle) * doubled)


def latitude_tables(height):
    column = jnp.arange(height, dtype=jnp.int32)[:, None]
    order = jnp.arange(height, dtype=jnp.int32)[None, :]
    angle = 2.0 * math.pi / height * (column * order % height).astype(jnp.float32)
    return (jnp.cos(angle), jnp.sin(angle))


def layer_norm(values, gain, shift):
    mean = jnp.sum(values, -1, keepdims=True) / values.shape[-1]
    spread = jnp.sum(values * values, -1, keepdims=True) / values.shape[-1] - mean * mean
    return (values - mean) * lax.rsqrt(spread + EPS) * gain + shift


def soft_shrink(values):
    return jnp.where(
        values > SHRINK, values - SHRINK, jnp.where(values < -SHRINK, values + SHRINK, 0.0)
    )


def block_apply(left, matrix):
    return jnp.einsum("bkmnj,nji->bkmni", left, matrix, precision=HIGH)


def spectral_mlp(real_part, imag_part, filter_in, filter_in_bias, filter_out, filter_out_bias):
    shape = real_part.shape
    blocks = filter_in.shape[1]
    size = filter_in.shape[2]
    real_blocks = real_part.reshape(shape[:-1] + (blocks, size))
    imag_blocks = imag_part.reshape(shape[:-1] + (blocks, size))
    first_real = jax.nn.relu(
        block_apply(real_blocks, filter_in[0])
        - block_apply(imag_blocks, filter_in[1])
        + filter_in_bias[0]
    )
    first_imag = jax.nn.relu(
        block_apply(imag_blocks, filter_in[0])
        + block_apply(real_blocks, filter_in[1])
        + filter_in_bias[1]
    )
    second_real = (
        block_apply(first_real, filter_out[0])
        - block_apply(first_imag, filter_out[1])
        + filter_out_bias[0]
    )
    second_imag = (
        block_apply(first_imag, filter_out[0])
        + block_apply(first_real, filter_out[1])
        + filter_out_bias[1]
    )
    return (soft_shrink(second_real).reshape(shape), soft_shrink(second_imag).reshape(shape))


def local(
    state,
    norm_gains,
    channel_biases,
    filter_in,
    filter_in_bias,
    filter_out,
    filter_out_bias,
    up_weight,
    up_bias,
    down_weight,
):
    width = state.shape[2]
    height = state.shape[1] * lax.axis_size("lat")
    scale = 1.0 / math.sqrt(height * width)
    lon_cos, lon_sin, back_cos, back_sin = longitude_tables(width, M)
    lat_cos, lat_sin = latitude_tables(height)
    gains = norm_gains.astype(jnp.float32)
    shifts = channel_biases.astype(jnp.float32)
    full_up, full_gains, full_biases = (
        lax.all_gather(up_weight, "ch", axis=1, tiled=True),
        *sent_together((norm_gains, channel_biases), "ch", 1, 0),
    )
    full_down, full_up_bias = sent_together_2((down_weight, up_bias), "ch", 0, 1)
    wide_gains = full_gains.astype(jnp.float32)
    wide_biases = full_biases.astype(jnp.float32)
    wide_up_bias = full_up_bias.astype(jnp.float32)
    values = state
    for step_index in range(STEPS):
        total, squares = in_one(
            (jnp.sum(values, -1, keepdims=True), jnp.sum(values * values, -1, keepdims=True)), "ch"
        )
        mean = total / D
        mean, spread = (mean, squares / D - mean * mean)
        normed = (values - mean) * lax.rsqrt(spread + EPS) * gains[0] + shifts[0]
        real_lon = jnp.einsum("bhwd,wm->bhmd", normed, lon_cos, precision=HIGH)
        imag_lon = -jnp.einsum("bhwd,wm->bhmd", normed, lon_sin, precision=HIGH)
        stacked = lax.all_to_all(
            jnp.stack((real_lon, imag_lon)), "lat", split_axis=3, concat_axis=2, tiled=True
        )
        spectral_real_lon = stacked[0]
        spectral_imag_lon = stacked[1]
        real_spec = (
            jnp.einsum("kh,bhmd->bkmd", lat_cos, spectral_real_lon, precision=HIGH)
            + jnp.einsum("kh,bhmd->bkmd", lat_sin, spectral_imag_lon, precision=HIGH)
        ) * scale
        imag_spec = (
            jnp.einsum("kh,bhmd->bkmd", lat_cos, spectral_imag_lon, precision=HIGH)
            - jnp.einsum("kh,bhmd->bkmd", lat_sin, spectral_real_lon, precision=HIGH)
        ) * scale
        out_real, out_imag = spectral_mlp(
            real_spec, imag_spec, filter_in, filter_in_bias, filter_out, filter_out_bias
        )
        real_rows = jnp.einsum("kh,bkmd->bhmd", lat_cos, out_real, precision=HIGH) - jnp.einsum(
            "kh,bkmd->bhmd", lat_sin, out_imag, precision=HIGH
        )
        imag_rows = jnp.einsum("kh,bkmd->bhmd", lat_cos, out_imag, precision=HIGH) + jnp.einsum(
            "kh,bkmd->bhmd", lat_sin, out_real, precision=HIGH
        )
        rows = lax.all_to_all(
            jnp.stack((real_rows, imag_rows)), "lat", split_axis=2, concat_axis=3, tiled=True
        )
        back = jnp.einsum("bhmd,wm->bhwd", rows[0], back_cos, precision=HIGH) - jnp.einsum(
            "bhmd,wm->bhwd", rows[1], back_sin, precision=HIGH
        )
        values = values + back * scale + normed
        owned = lax.all_to_all(values, "ch", split_axis=2, concat_axis=3, tiled=True)
        normed_two = layer_norm(owned, wide_gains[1], wide_biases[1]).astype(jnp.bfloat16)
        flat = normed_two.reshape(-1, normed_two.shape[-1])
        pre = jnp.dot(flat, full_up, preferred_element_type=jnp.float32) + wide_up_bias
        hidden = jax.nn.gelu(pre, approximate=False).astype(jnp.bfloat16)
        mixed = jnp.dot(hidden, full_down, preferred_element_type=jnp.float32) + wide_biases[2]
        values = values + lax.all_to_all(
            mixed.reshape(owned.shape), "ch", split_axis=3, concat_axis=2, tiled=True
        )
    return values


def solution(mesh):
    placed = (
        P(None, "lat", None, "ch"),
        P(None, "ch"),
        P(None, "ch"),
        P(None, "ch", None, None),
        P(None, "ch", None),
        P(None, "ch", None, None),
        P(None, "ch", None),
        P(None, "ch"),
        P("ch"),
        P("ch", None),
    )
    return jax.shard_map(
        local, mesh=mesh, in_specs=placed, out_specs=P(None, "lat", None, "ch"), check_vma=False
    )
```

profile of v0, /device:TPU:4, one launch (start us, length us, event | category | flops | bytes accessed | tf_op | source)
XLA Modules:
  0.0 492.6 jit_solution(10476422988369624664)
XLA Ops:
  7.4 2.5 pad_maximum_fusion
  10.0 2.7 fusion.998
  13.5 4.8 all-to-all-start
  19.1 2.2 all-to-all-done
  24.3 8.6 %all-to-all-start.1 = ((f32[2,1,3,64,192]{4,0,2,1,3:T(2,128)}), f32[2,1,3,64,192]{4,0,2,1,3:T(2,128)S(1)}, u32[]{:S(2)}, u32[]{:S(2)}) async-start(f32[2,1,3,64,192]{4,0,2,1,3:T(2,128)} %copy.412), calls=%async_computation.1 | async-start | bytes 786432 | tf_op jit(solution)/shard_map/all_to_all | solution.py:157
  33.0 10.1 %all-to-all-done.1 = f32[2,1,3,64,192]{4,0,2,1,3:T(2,128)S(1)} async-done(((f32[2,1,3,64,192]{4,0,2,1,3:T(2,128)}), f32[2,1,3,64,192]{4,0,2,1,3:T(2,128)S(1)}, u32[]{:S(2)}, u32[]{:S(2)}) %all-to-all-start.1) | async-done | bytes 294944 | tf_op jit(solution)/shard_map/all_to_all | solution.py:157
  52.5 3.9 all-to-all-start.2
  56.4 12.6 %all-gather = bf16[4,192,5]{1,2,0:T(8,128)(2,1)S(1)} all-gather(bf16[1,192,5]{1,2,0:T(8,128)(2,1)S(1)} %maximum_bitcast_fusion), channel_id=1, replica_groups=mesh['lat'=32,'ch'=4] {'ch'}, dimensions={0}, use_global_device_ids=true | all-gather | bytes 9600 | tf_op jit(solution)/shard_map/all_gather | solution.py:41
  73.0 6.0 %all-to-all-start.3 = ((f32[1,3,180,192]{3,0,1,2:T(1,128)}), f32[1,3,180,192]{3,0,1,2:T(1,128)S(1)}, u32[]{:S(2)}, u32[]{:S(2)}) async-start(f32[1,3,180,192]{3,0,1,2:T(1,128)} %copy.429), calls=%async_computation.3 | async-start | bytes 1105920 | tf_op jit(solution)/shard_map/all_to_all | solution.py:186
  79.1 5.6 %all-to-all-done.3 = f32[1,3,180,192]{3,0,1,2:T(1,128)S(1)} async-done(((f32[1,3,180,192]{3,0,1,2:T(1,128)}), f32[1,3,180,192]{3,0,1,2:T(1,128)S(1)}, u32[]{:S(2)}, u32[]{:S(2)}) %all-to-all-start.3) | async-done | bytes 414752 | tf_op jit(solution)/shard_map/all_to_all | solution.py:186
  88.5 37.1 %all-gather.4.cloned.1.call-done = bf16[768,3072]{1,0:T(8,128)(2,1)} async-done(((bf16[768,768]{1,0:T(8,128)(2,1)}), bf16[768,3072]{1,0:T(8,128)(2,1)}) %all-gather.4.cloned.1.call-update) | async-done | bytes 4718608 | tf_op jit(solution)/shard_map/all_gather | solution.py:140
  125.6 7.5 %fusion.64 = f32[135,768]{1,0:T(8,128)S(1)} fusion(bf16[3072,769]{1,0:T(8,128)(2,1)} %all-gather.6.cloned.1.call-done, bf16[768,3072]{1,0:T(8,128)(2,1)} %all-gather.4.cloned.1.call-done, f32[3072]{0:T(1024)S(1)} %convert_reduce_fusion, f32[135,768]{1,0:T(8,128)S(1)} %all_to_all.218, f32[768]{0:T(1024)S(1)} %get-tuple-element.22, ...), kind=kOutput, calls=%fused_computation.110 | convolution fusion | flops 1302013440 | bytes 10289208 | tf_op jit(solution)/shard_map/dot_general | solution.py:191
  133.1 2.6 copy.434
  136.3 5.2 %reduce.44 = f32[768,3,45]{2,1,0:T(4,128)S(1)} reduce(f32[768,3,1,45]{3,2,1,0:T(1,128)} %bitcast.731, f32[]{:T(128)} %broadcast.1087), dimensions={2}, to_apply=%bitcast.643.reduce_sub_computation | reduce | bytes 829444
  143.1 10.5 %all_to_all.288 = f32[4,1,25920]{2,1,0:T(1,128)S(1)} all-to-all(f32[4,1,25920]{2,1,0:T(1,128)S(1)} %reshape.1007), channel_id=1, replica_groups=mesh['lat'=32,'ch'=4] {'ch'}, dimensions={0} | all-to-all | bytes 829440 | tf_op jit(solution)/shard_map/all_to_all | solution.py:192
  155.5 3.3 reshape.1008
  158.7 4.9 bitcast_reduce_fusion.3
  165.7 7.7 %all_to_all.289 = f32[4,1,1080]{2,1,0:T(1,128)S(1)} all-to-all(f32[4,1,1080]{2,1,0:T(1,128)S(1)} %broadcast_in_dim.28), channel_id=1, replica_groups=mesh['lat'=32,'ch'=4] {'ch'}, dimensions={0} | all-to-all | bytes 34560 | tf_op jit(solution)/shard_map/all_to_all | solution.py:20
  175.8 17.5 %all_to_all.290 = f32[2,1,3,64,192]{4,0,2,1,3:T(2,128)S(1)} all-to-all(f32[2,1,3,64,192]{4,0,2,1,3:T(2,128)S(1)} %copy.439), channel_id=1, replica_groups=mesh['lat'=32,'ch'=4] {'lat'}, dimensions={3} | all-to-all | bytes 589824 | tf_op jit(solution)/shard_map/all_to_all | solution.py:157
  201.9 13.6 %all_to_all.291 = f32[2,1,96,2,192]{4,3,1,0,2:T(2,128)S(1)} all-to-all(f32[2,1,96,2,192]{4,3,1,0,2:T(2,128)S(1)} %copy.451), channel_id=1, replica_groups=mesh['lat'=32,'ch'=4] {'lat'}, dimensions={2} | all-to-all | bytes 589824 | tf_op jit(solution)/shard_map/all_to_all | solution.py:179
  218.6 13.2 %all_to_all.292 = f32[1,3,180,192]{3,0,1,2:T(1,128)S(1)} all-to-all(f32[1,3,180,192]{3,0,1,2:T(1,128)S(1)} %copy.455), channel_id=1, replica_groups=mesh['lat'=32,'ch'=4] {'ch'}, dimensions={2} | all-to-all | bytes 829440 | tf_op jit(solution)/shard_map/all_to_all | solution.py:186
  234.1 7.5 %fusion.67 = f32[135,768]{1,0:T(8,128)S(1)} fusion(bf16[3072,769]{1,0:T(8,128)(2,1)} %all-gather.6.cloned.1.call-done, bf16[768,3072]{1,0:T(8,128)(2,1)} %all-gather.4.cloned.1.call-done, f32[3072]{0:T(1024)S(1)} %convert_reduce_fusion, f32[135,768]{1,0:T(8,128)S(1)} %all_to_all.233, f32[135]{0:T(256)S(1)} %add_rsqrt_fusion.6, f32[135]{0:T(256)S(1)} %div.93, ...), kind=kOutput, calls=%fused_computation.111 | convolution fusion | flops 1302013440 | bytes 10289208 | tf_op jit(solution)/shard_map/dot_general | solution.py:191
  241.7 2.6 copy.458
  244.3 5.2 %reduce.46 = f32[768,3,45]{2,1,0:T(4,128)S(1)} reduce(f32[768,3,1,45]{3,2,1,0:T(1,128)} %bitcast.732, f32[]{:T(128)} %broadcast.1087), dimensions={2}, to_apply=%bitcast.645.reduce_sub_computation | reduce | bytes 829444
  251.1 10.4 %all_to_all.293 = f32[4,1,25920]{2,1,0:T(1,128)S(1)} all-to-all(f32[4,1,25920]{2,1,0:T(1,128)S(1)} %reshape.1009), channel_id=1, replica_groups=mesh['lat'=32,'ch'=4] {'ch'}, dimensions={0} | all-to-all | bytes 829440 | tf_op jit(solution)/shard_map/all_to_all | solution.py:192
  261.6 1.9 reduce.47
  263.5 3.3 reshape.1010
  266.7 4.9 bitcast_reduce_fusion.2
  273.7 7.7 %all_to_all.294 = f32[4,1,1080]{2,1,0:T(1,128)S(1)} all-to-all(f32[4,1,1080]{2,1,0:T(1,128)S(1)} %broadcast_in_dim.29), channel_id=1, replica_groups=mesh['lat'=32,'ch'=4] {'ch'}, dimensions={0} | all-to-all | bytes 34560 | tf_op jit(solution)/shard_map/all_to_all | solution.py:20
  283.7 15.0 %all_to_all.295 = f32[2,1,3,64,192]{4,0,2,1,3:T(2,128)S(1)} all-to-all(f32[2,1,3,64,192]{4,0,2,1,3:T(2,128)S(1)} %copy.463), channel_id=1, replica_groups=mesh['lat'=32,'ch'=4] {'lat'}, dimensions={3} | all-to-all | bytes 589824 | tf_op jit(solution)/shard_map/all_to_all | solution.py:157
  307.3 13.6 %all_to_all.296 = f32[2,1,96,2,192]{4,3,1,0,2:T(2,128)S(1)} all-to-all(f32[2,1,96,2,192]{4,3,1,0,2:T(2,128)S(1)} %copy.475), channel_id=1, replica_groups=mesh['lat'=32,'ch'=4] {'lat'}, dimensions={2} | all-to-all | bytes 589824 | tf_op jit(solution)/shard_map/all_to_all | solution.py:179
  324.0 13.2 %all_to_all.297 = f32[1,3,180,192]{3,0,1,2:T(1,128)S(1)} all-to-all(f32[1,3,180,192]{3,0,1,2:T(1,128)S(1)} %copy.479), channel_id=1, replica_groups=mesh['lat'=32,'ch'=4] {'ch'}, dimensions={2} | all-to-all | bytes 829440 | tf_op jit(solution)/shard_map/all_to_all | solution.py:186
  339.5 7.5 %fusion.70 = f32[135,768]{1,0:T(8,128)S(1)} fusion(bf16[3072,769]{1,0:T(8,128)(2,1)} %all-gather.6.cloned.1.call-done, bf16[768,3072]{1,0:T(8,128)(2,1)} %all-gather.4.cloned.1.call-done, f32[3072]{0:T(1024)S(1)} %convert_reduce_fusion, f32[135,768]{1,0:T(8,128)S(1)} %all_to_all.248, f32[135]{0:T(256)S(1)} %add_rsqrt_fusion.5, f32[135]{0:T(256)S(1)} %div.101, ...), kind=kOutput, calls=%fused_computation.112 | convolution fusion | flops 1302013440 | bytes 10289208 | tf_op jit(solution)/shard_map/dot_general | solution.py:191
  347.1 2.6 copy.482
  349.8 5.2 %reduce.48 = f32[768,3,45]{2,1,0:T(4,128)S(1)} reduce(f32[768,3,1,45]{3,2,1,0:T(1,128)} %bitcast.733, f32[]{:T(128)} %broadcast.1087), dimensions={2}, to_apply=%bitcast.647.reduce_sub_computation | reduce | bytes 829444
  356.6 10.4 %all_to_all.298 = f32[4,1,25920]{2,1,0:T(1,128)S(1)} all-to-all(f32[4,1,25920]{2,1,0:T(1,128)S(1)} %reshape.1011), channel_id=1, replica_groups=mesh['lat'=32,'ch'=4] {'ch'}, dimensions={0} | all-to-all | bytes 829440 | tf_op jit(solution)/shard_map/all_to_all | solution.py:192
  368.9 3.3 reshape.1012
  372.2 4.9 bitcast_reduce_fusion.1
  379.2 7.7 %all_to_all.299 = f32[4,1,1080]{2,1,0:T(1,128)S(1)} all-to-all(f32[4,1,1080]{2,1,0:T(1,128)S(1)} %broadcast_in_dim.30), channel_id=1, replica_groups=mesh['lat'=32,'ch'=4] {'ch'}, dimensions={0} | all-to-all | bytes 34560 | tf_op jit(solution)/shard_map/all_to_all | solution.py:20
  389.2 15.0 %all_to_all.300 = f32[2,1,3,64,192]{4,0,2,1,3:T(2,128)S(1)} all-to-all(f32[2,1,3,64,192]{4,0,2,1,3:T(2,128)S(1)} %copy.487), channel_id=1, replica_groups=mesh['lat'=32,'ch'=4] {'lat'}, dimensions={3} | all-to-all | bytes 589824 | tf_op jit(solution)/shard_map/all_to_all | solution.py:157
  412.8 13.6 %all_to_all.301 = f32[2,1,96,2,192]{4,3,1,0,2:T(2,128)S(1)} all-to-all(f32[2,1,96,2,192]{4,3,1,0,2:T(2,128)S(1)} %copy.499), channel_id=1, replica_groups=mesh['lat'=32,'ch'=4] {'lat'}, dimensions={2} | all-to-all | bytes 589824 | tf_op jit(solution)/shard_map/all_to_all | solution.py:179
  429.5 13.2 %all_to_all.302 = f32[1,3,180,192]{3,0,1,2:T(1,128)S(1)} all-to-all(f32[1,3,180,192]{3,0,1,2:T(1,128)S(1)} %copy.503), channel_id=1, replica_groups=mesh['lat'=32,'ch'=4] {'ch'}, dimensions={2} | all-to-all | bytes 829440 | tf_op jit(solution)/shard_map/all_to_all | solution.py:186
  445.0 7.5 %fusion.73 = f32[135,768]{1,0:T(8,128)S(1)} fusion(bf16[3072,769]{1,0:T(8,128)(2,1)} %all-gather.6.cloned.1.call-done, bf16[768,3072]{1,0:T(8,128)(2,1)} %all-gather.4.cloned.1.call-done, f32[3072]{0:T(1024)S(1)} %convert_reduce_fusion, f32[135,768]{1,0:T(8,128)S(1)} %all_to_all.263, f32[135]{0:T(256)S(1)} %add_rsqrt_fusion.4, f32[135]{0:T(256)S(1)} %div.109, ...), kind=kOutput, calls=%fused_computation.113 | convolution fusion | flops 1302013440 | bytes 10289208 | tf_op jit(solution)/shard_map/dot_general | solution.py:191
  452.6 2.6 copy.506
  455.2 5.2 %reduce.50 = f32[768,3,45]{2,1,0:T(4,128)S(1)} reduce(f32[768,3,1,45]{3,2,1,0:T(1,128)} %bitcast.734, f32[]{:T(128)} %broadcast.1087), dimensions={2}, to_apply=%bitcast.649.reduce_sub_computation | reduce | bytes 829444
  462.0 10.4 %all_to_all.303 = f32[4,1,25920]{2,1,0:T(1,128)S(1)} all-to-all(f32[4,1,25920]{2,1,0:T(1,128)S(1)} %reshape.1013), channel_id=1, replica_groups=mesh['lat'=32,'ch'=4] {'ch'}, dimensions={0} | all-to-all | bytes 829440 | tf_op jit(solution)/shard_map/all_to_all | solution.py:192
  474.4 3.3 reshape.1014
  477.6 4.9 bitcast_reduce_fusion
  (277 shorter events, 92.4 us)
Async XLA Ops:
  6.5 80.5 %all-gather.6.cloned.1.call-start = ((), (), s32[]{:S(2)}) async-start(), calls=%async_computation.21 | async-start | bytes 6881280 | tf_op jit(solution)/shard_map/all_gather | solution.py:53
  7.4 2.6 copy-start.2
  9.9 9.1 %copy-start.3 = (bf16[3,192]{1,0:T(4,128)(2,1)S(1)}, bf16[3,192]{1,0:T(4,128)(2,1)}, u32[]{:S(2)}) copy-start(bf16[3,192]{1,0:T(4,128)(2,1)} %param.12) | copy-start | bytes 3460
  9.9 9.1 %copy-start.4 = (bf16[2,192]{1,0:T(2,128)(2,1)S(1)}, bf16[2,192]{1,0:T(2,128)(2,1)}, u32[]{:S(2)}) copy-start(bf16[2,192]{1,0:T(2,128)(2,1)} %param.11) | copy-start | bytes 2308
  13.5 7.8 %all-to-all-start = ((f32[4,1,1080]{2,1,0:T(1,128)}), f32[4,1,1080]{2,1,0:T(1,128)S(1)}, u32[]{:S(2)}, u32[]{:S(2)}) async-start(f32[4,1,1080]{2,1,0:T(1,128)} %broadcast_in_dim.27), calls=%async_computation | async-start | bytes 36864 | tf_op jit(solution)/shard_map/all_to_all | solution.py:20
  18.3 107.3 %all-gather.4.cloned.1.call-start = ((), (), s32[]{:S(2)}) async-start(), calls=%async_computation.20 | async-start | bytes 5898240 | tf_op jit(solution)/shard_map/all_gather | solution.py:140
  22.4 10.6 %copy-start.5 = (f32[2,2,96]{2,1,0:T(2,128)S(1)}, f32[2,2,96]{2,1,0:T(2,128)}, u32[]{:S(2)}) copy-start(f32[2,2,96]{2,1,0:T(2,128)} %param.14) | copy-start | bytes 4612
  22.4 10.6 %copy-start.6 = (f32[2,2,96]{2,1,0:T(2,128)S(1)}, f32[2,2,96]{2,1,0:T(2,128)}, u32[]{:S(2)}) copy-start(f32[2,2,96]{2,1,0:T(2,128)} %param.16) | copy-start | bytes 4612
  24.3 18.8 %all-to-all-start.1 = ((f32[2,1,3,64,192]{4,0,2,1,3:T(2,128)}), f32[2,1,3,64,192]{4,0,2,1,3:T(2,128)S(1)}, u32[]{:S(2)}, u32[]{:S(2)}) async-start(f32[2,1,3,64,192]{4,0,2,1,3:T(2,128)} %copy.412), calls=%async_computation.1 | async-start | bytes 786432 | tf_op jit(solution)/shard_map/all_to_all | solution.py:157
  43.3 2.0 copy-start
  44.7 3.1 copy-start.1
  52.5 16.6 %all-to-all-start.2 = ((f32[2,1,96,2,192]{4,3,1,0,2:T(2,128)}), f32[2,1,96,2,192]{4,3,1,0,2:T(2,128)S(1)}, u32[]{:S(2)}, u32[]{:S(2)}) async-start(f32[2,1,96,2,192]{4,3,1,0,2:T(2,128)} %copy.424), calls=%async_computation.2 | async-start | bytes 786432 | tf_op jit(solution)/shard_map/all_to_all | solution.py:179
  73.0 11.7 %all-to-all-start.3 = ((f32[1,3,180,192]{3,0,1,2:T(1,128)}), f32[1,3,180,192]{3,0,1,2:T(1,128)S(1)}, u32[]{:S(2)}, u32[]{:S(2)}) async-start(f32[1,3,180,192]{3,0,1,2:T(1,128)} %copy.429), calls=%async_computation.3 | async-start | bytes 1105920 | tf_op jit(solution)/shard_map/all_to_all | solution.py:186
Sparse Core Ops, SparseCore 0:
  10.1 60.8 all-gather.5
  72.6 52.9 all-gather.3
where the time goes:
time: 500 us; the launch traced here: 493 us
  blocking collectives  205 us (41%)
  local copies, waits for them, and re-layouts  76.7 us (15%)
  matrix products  74 us (15%)
  waiting for transfers between devices  55.8 us (11%)
  other arithmetic  42.1 us (8%)
  starting transfers between devices  23.3 us (5%)
  between operations  15.2 us (3%)
    all_to_all x3, blocking collectives, local(): lax.all_to_all(jnp.stack((real_lon, imag_lon)), 'lat', split_axis=3, conc...  47.4 us
    all_to_all x4, blocking collectives, local(): lax.all_to_all(mixed.reshape(owned.shape), 'ch', split_axis=3, concat_axi...  41.8 us
    all_to_all x3, blocking collectives, local(): lax.all_to_all(jnp.stack((real_rows, imag_rows)), 'lat', split_axis=2, co...  40.9 us
    all_to_all x3, blocking collectives, local(): lax.all_to_all(values, 'ch', split_axis=2, concat_axis=3, tiled=True)  39.6 us
    all_gather x1, waiting for transfers between devices, local(): lax.all_gather(up_weight, 'ch', axis=1, tiled=True)  37.1 us
    dot_general x4, matrix products, local(): jnp.dot(hidden, full_down, preferred_element_type=jnp.float32)  30 us
    all_to_all x12, local copies, waits for them, and re-layouts, local(): lax.all_to_all(mixed.reshape(owned.shape), 'ch', split_axis=3, concat_axi...  25.7 us
    all_to_all x3, blocking collectives, sent_to_all(): lax.all_to_all(jnp.broadcast_to(shard[None], (length, *shard.shape)), axi...  23.2 us
  transfers between devices with their start and end apart: 6, of which 4 were waited for; matrix products, arithmetic and copies ran while one was open for 5% of the time, Pallas kernels for 0%

commit v1 on v0

v1 whole, which is shorter than its diff:
```python
import math

import jax
import jax.numpy as jnp
import numpy as np
from jax import lax
from jax.experimental import pallas as pl
from jax.experimental.pallas import tpu as pltpu
from jax.sharding import PartitionSpec as P

D = 768
FF = 3072
W = 180
R = 192
H = 96
M = 64
NB = 8
BS = 96
STEPS = 4
NL = 32
NC = 4
ND = NL * NC
OWN = 3
G = 16
SCALE = 1.0 / math.sqrt(H * W)
EPS = 1e-05
SHRINK = 0.01
MESH = pl.DeviceIdType.MESH
BF = jnp.bfloat16
F32 = jnp.float32


def tables():
    modes = np.arange(M)
    w = np.arange(W)
    ang = 2.0 * np.pi / W * ((w[:, None] * modes[None, :]) % W)
    c, s = np.cos(ang), np.sin(ang)
    dbl = np.where(modes == 0, 1.0, 2.0)
    fwd = np.zeros((G, 2, 4, R))
    fwd[:, 0, :, :W] = c.T.reshape(G, 4, W)
    fwd[:, 1, :, :W] = -s.T.reshape(G, 4, W)
    back = np.zeros((R, G, 2, 4))
    back[:W, :, 0, :] = (c * dbl).reshape(W, G, 4)
    back[:W, :, 1, :] = -(s * dbl).reshape(W, G, 4)
    h = np.arange(H)
    ang = 2.0 * np.pi / H * ((h[:, None] * h[None, :]) % H)
    c, s = np.cos(ang), np.sin(ang)
    lat = np.zeros((2, H, H, 2))
    lat[0, :, :, 0] = c
    lat[0, :, :, 1] = s
    lat[1, :, :, 0] = -s
    lat[1, :, :, 1] = c
    lat = lat.reshape(192, 192)
    fwd, back = halves(fwd.reshape(128, R)), halves(back.reshape(R, 128))
    return (
        np.concatenate([fwd[0], fwd[1], fwd[0]], axis=1),
        np.concatenate(back, axis=1),
        np.stack(halves(lat)),
        np.stack(halves(lat.T)),
    )


def halves(a):
    a = np.asarray(a, np.float32)
    hi = a.astype(BF)
    return hi, (a - hi.astype(np.float32)).astype(BF)


def parts(v):
    hi = v.astype(BF)
    return hi, (v - hi.astype(F32)).astype(BF)


def spread_out(t_ref, o_ref):
    def iota(shape, dim):
        return lax.broadcasted_iota(jnp.int32, shape, dim)

    one = lambda m: jnp.where(m, 1.0, 0.0).astype(BF)
    rows = one(iota((768, 192), 0) // 4 == iota((768, 192), 1))
    cols = one(iota((192, 768), 1) // 4 == iota((192, 768), 0))
    keep = lax.rem(iota((192, 768), 0), 4) == lax.rem(iota((192, 768), 1), 4)
    for half in range(2):
        tall = jnp.dot(rows, t_ref[half], preferred_element_type=F32).astype(BF)
        for j in range(4):
            wide = jnp.dot(tall[j * 192:(j + 1) * 192], cols, preferred_element_type=F32)
            o_ref[half, j * 192:(j + 1) * 192, :] = jnp.where(keep, wide, 0.0).astype(BF)


def norm(v, gain, shift):
    mean = jnp.sum(v, -1, keepdims=True) / D
    spread = jnp.sum(v * v, -1, keepdims=True) / D - mean * mean
    return (v - mean) * lax.rsqrt(spread + EPS) * gain + shift


def kernel(
    state, small, fin, finb, fout, foutb, up, down, fwd, back, t_to, t_fro,
    out,
    xin, smalls, x, nb, fsend, frecv, bsend, brecv, w1, b1, w2, b2, par, hid, lat_to, lat_fro, n3,
    in_s, in_r, sm_s, sm_r, f_s, f_r, b_s, b_r, o_s, o_r,
):
    l = lax.axis_index("lat")
    c = lax.axis_index("ch")
    me = l * NC + c
    row = l * OWN + c
    blk = lax.rem(l, 2)
    owner = c < OWN

    def to_owner(i):
        return (
            pltpu.make_async_remote_copy(
                state.at[i], xin.at[c], in_s.at[i], in_r.at[c],
                device_id=(l, i), device_id_type=MESH),
            pltpu.make_async_remote_copy(
                small, smalls.at[c], sm_s.at[i], sm_r.at[c],
                device_id=(l, i), device_id_type=MESH),
        )

    for i in range(OWN):
        @pl.when(c != i)
        def _(i=i):
            a, b = to_owner(i)
            a.start()
            b.start()

        @pl.when(c == i)
        def _(i=i):
            pltpu.make_async_copy(state.at[i], xin.at[i], in_r.at[i]).start()
            pltpu.make_async_copy(small, smalls.at[i], sm_r.at[i]).start()

    for w_ref, b_ref, src, bsrc in ((w1, b1, fin, finb), (w2, b2, fout, foutb)):
        w_ref[...] = jnp.zeros_like(w_ref)
        b_ref[...] = jnp.zeros_like(b_ref)
        for at, re, im in zip((0, 256), parts(src[0, blk]), parts(src[1, blk])):
            w_ref[at:at + BS, 0:BS] = re
            w_ref[at:at + BS, 128:128 + BS] = im
            w_ref[at + 128:at + 128 + BS, 0:BS] = -im
            w_ref[at + 128:at + 128 + BS, 128:128 + BS] = re
        w_ref[512:768, :] = w_ref[0:256, :]
        b_ref[:, 0:BS] = bsrc[0, pl.ds(blk, 1), :]
        b_ref[:, 128:128 + BS] = bsrc[1, pl.ds(blk, 1), :]

    spread_out(t_to, lat_to)
    spread_out(t_fro, lat_fro)

    @pl.when(owner)
    def _():
        for j in range(NC):
            pltpu.make_async_copy(xin.at[j], xin.at[j], in_r.at[j]).wait()
            pltpu.make_async_copy(smalls.at[j], smalls.at[j], sm_r.at[j]).wait()
        par[0:5, :] = jnp.concatenate([smalls[j, 0:5, 0:192] for j in range(NC)], axis=1)
        x[0:W, :] = jnp.concatenate([xin[j] for j in range(NC)], axis=1)
        x[W:R, :] = jnp.zeros((R - W, D), F32)
        fsend[...] = jnp.zeros_like(fsend)

    for i in range(OWN):
        @pl.when(c != i)
        def _(i=i):
            a, b = to_owner(i)
            a.wait_send()
            b.wait_send()

    def step(s, carry):
        @pl.when(owner)
        def _():
            v = x[...]
            n = norm(v, par[0:1, :], par[2:3, :])
            x[...] = v + n
            hi, lo = parts(n)
            n3[0:R, :] = hi
            n3[R:2 * R, :] = hi
            n3[2 * R:3 * R, :] = lo
            lon = jnp.dot(fwd[...], n3[...], preferred_element_type=F32)
            for b in range(NB):
                fsend[b, :, :, 0:BS] = lon[:, b * BS:(b + 1) * BS].reshape(G, 8, BS).astype(BF)

            def send(i, carry):
                d = lax.rem(me + i, ND)
                dl, dc = d // NC, lax.rem(d, NC)
                src = fsend.at[2 * dc + lax.rem(dl, 2), dl // 2]

                pltpu.make_async_remote_copy(
                    src, frecv.at[row], f_s, f_r, device_id=(dl, dc), device_id_type=MESH).start()
                return carry

            lax.fori_loop(1, ND, send, 0)
            pltpu.make_async_copy(
                fsend.at[2 * c + blk, l // 2], frecv.at[row], f_r).start()

        pltpu.make_async_copy(frecv, frecv, f_r).wait()
        got = frecv[...].reshape(H * 8, 128)
        spec = jnp.dot(lat_to[0], got, preferred_element_type=F32)
        spec = (spec + jnp.dot(lat_to[1], got, preferred_element_type=F32)) * SCALE
        spec = jnp.concatenate([spec[0:384], spec[384:768]], axis=1)
        hi, lo = parts(spec)
        first = jnp.dot(jnp.concatenate([hi, hi, lo], axis=1), w1[...], preferred_element_type=F32) + b1[...]
        hi, lo = parts(jnp.maximum(first, 0.0))
        second = jnp.dot(jnp.concatenate([hi, hi, lo], axis=1), w2[...], preferred_element_type=F32) + b2[...]
        second = jnp.where(second > SHRINK, second - SHRINK,
                           jnp.where(second < -SHRINK, second + SHRINK, 0.0))
        hi, lo = parts(jnp.concatenate([second[:, 0:128], second[:, 128:256]], axis=0))
        both = jnp.dot(lat_fro[0], jnp.concatenate([hi, lo], axis=1), preferred_element_type=F32)
        rows = jnp.dot(lat_fro[1], hi, preferred_element_type=F32)
        rows = (rows + both[:, 0:128] + both[:, 128:256]).astype(BF)
        bsend[...] = rows.reshape(H, 8, 128)

        def sendb(i, carry):
            dl = lax.rem(l + i, NL)
            for dc in range(OWN):
                @pl.when(jnp.logical_or(dl != l, c != dc))
                def _():
                    pltpu.make_async_remote_copy(
                        bsend.at[dl * OWN + dc], brecv.at[2 * c + blk, l // 2], b_s, b_r,
                        device_id=(dl, dc), device_id_type=MESH).start()
            return carry

        lax.fori_loop(0, NL, sendb, 0)

        @pl.when(owner)
        def _():
            pltpu.make_async_copy(bsend.at[row], brecv.at[2 * c + blk, l // 2], b_r).start()
            pltpu.make_async_copy(brecv, brecv, b_r).wait()
            packed = jnp.concatenate(
                [brecv[b].reshape(128, 128)[:, 0:BS].astype(F32) for b in range(NB)], axis=1).astype(BF)
            packed = jnp.concatenate([packed, packed], axis=0)
            v = x[...] + jnp.dot(back[...], packed, preferred_element_type=F32) * SCALE
            x[...] = v
            nb[...] = norm(v, par[1:2, :], par[3:4, :]).astype(BF)
            for q in range(NC):
                for j in range(3):
                    pre = jnp.dot(nb[...], up[:, q * 768 + j * 256:q * 768 + (j + 1) * 256], preferred_element_type=F32)
                    pre = pre + smalls[q, 5:6, j * 256:(j + 1) * 256]
                    act = 0.5 * pre * (1.0 + lax.erf(pre * math.sqrt(0.5)))
                    hid[:, q * 768 + j * 256:q * 768 + (j + 1) * 256] = act.astype(BF)
            for j in range(3):
                cols = slice(j * 256, (j + 1) * 256)
                mixed = jnp.dot(hid[...], down[:, cols], preferred_element_type=F32)
                x[:, cols] = x[:, cols] + mixed + par[4:5, cols]
            pltpu.make_async_copy(fsend.at[0:7], fsend.at[0:7], f_s).wait()
            pltpu.make_async_copy(fsend.at[7, 0:15], fsend.at[7, 0:15], f_s).wait()
            pltpu.make_async_copy(bsend.at[0:95], bsend.at[0:95], b_s).wait()

        @pl.when(jnp.logical_not(owner))
        def _():
            pltpu.make_async_copy(bsend, bsend, b_s).wait()

        return carry

    lax.fori_loop(0, STEPS, step, 0)

    @pl.when(owner)
    def _():
        for j in range(NC):
            xin[j] = x[0:W, j * 192:(j + 1) * 192]

        for j in range(NC):
            @pl.when(c != j)
            def _(j=j):
                pltpu.make_async_remote_copy(
                    xin.at[j], out.at[c], o_s.at[j], o_r.at[c],
                    device_id=(l, j), device_id_type=MESH).start()

            @pl.when(c == j)
            def _(j=j):
                pltpu.make_async_copy(xin.at[j], out.at[c], o_r.at[c]).start()

    for i in range(OWN):
        pltpu.make_async_copy(out.at[i], out.at[i], o_r.at[i]).wait()

    @pl.when(owner)
    def _():
        for j in range(NC):
            @pl.when(c != j)
            def _(j=j):
                pltpu.make_async_copy(xin.at[j], xin.at[j], o_s.at[j]).wait()


def local(
    state, norm_gains, channel_biases, filter_in, filter_in_bias, filter_out, filter_out_bias,
    up_weight, up_bias, down_weight,
):
    up = lax.all_gather(up_weight, "ch", axis=1, tiled=True)
    down = lax.all_gather(down_weight, "ch", axis=0, tiled=True)
    small = jnp.zeros((8, D), F32)
    small = small.at[0:2, 0:192].set(norm_gains.astype(F32))
    small = small.at[2:5, 0:192].set(channel_biases.astype(F32))
    small = small.at[5, :].set(up_bias.astype(F32))
    fwd, back, t_to, t_fro = tables()
    vm = pl.BlockSpec(memory_space=pltpu.VMEM)
    anyspace = pl.BlockSpec(memory_space=pl.ANY)
    sem = pltpu.SemaphoreType.DMA
    result = pl.pallas_call(
        kernel,
        out_shape=jax.ShapeDtypeStruct((OWN, W, 192), F32),
        in_specs=[anyspace, vm] + [vm] * 10,
        out_specs=vm,
        scratch_shapes=[
            pltpu.VMEM((NC, W, 192), F32),
            pltpu.VMEM((NC, 8, D), F32),
            pltpu.VMEM((R, D), F32),
            pltpu.VMEM((R, D), BF),
            pltpu.VMEM((NB, G, 8, 128), BF),
            pltpu.VMEM((H, 8, 128), BF),
            pltpu.VMEM((H, 8, 128), BF),
            pltpu.VMEM((NB, G, 8, 128), BF),
            pltpu.VMEM((768, 256), BF),
            pltpu.VMEM((1, 256), F32),
            pltpu.VMEM((768, 256), BF),
            pltpu.VMEM((1, 256), F32),
            pltpu.VMEM((8, D), F32),
            pltpu.VMEM((R, FF), BF),
            pltpu.VMEM((2, 768, 768), BF),
            pltpu.VMEM((2, 768, 768), BF),
            pltpu.VMEM((3 * R, D), BF),
            sem((OWN,)), sem((NC,)), sem((OWN,)), sem((NC,)),
            sem, sem, sem, sem, sem((NC,)), sem((OWN,)),
        ],
        compiler_params=pltpu.CompilerParams(
            has_side_effects=True, vmem_limit_bytes=50 * 1024 * 1024),
        name="rollout",
    )(
        state[0], small, filter_in, filter_in_bias, filter_out, filter_out_bias,
        up, down, jnp.asarray(fwd), jnp.asarray(back), jnp.asarray(t_to), jnp.asarray(t_fro),
    )
    return result[None]


def solution(mesh):
    placed = (
        P(None, "lat", None, "ch"),
        P(None, "ch"),
        P(None, "ch"),
        P(None, "ch", None, None),
        P(None, "ch", None),
        P(None, "ch", None, None),
        P(None, "ch", None),
        P(None, "ch"),
        P("ch"),
        P("ch", None),
    )
    return jax.shard_map(
        local, mesh=mesh, in_specs=placed, out_specs=P(None, "lat", None, "ch"), check_vma=False
    )
```

time: 500 us -> 257 us (0.51); the launches traced: 493 us -> 257 us
  blocking collectives: 205 us -> 0 us
  Pallas kernels: 0 us -> 124 us
  matrix products: 74 us -> 0 us
  local copies, waits for them, and re-layouts: 76.7 us -> 10.4 us
  waiting for transfers between devices: 55.8 us -> 108 us
  other arithmetic: 42.1 us -> 1.37 us
  starting transfers between devices: 23.3 us -> 0.04 us
    all_to_all x16 -> x0, blocking collectives: 193 us -> none  [the longest x3 47.4 us: local(): lax.all_to_all(jnp.stack((real_lon, imag_lon)), 'lat', split_axis=3, conc...]
    pallas_call x0 -> x1, Pallas kernels: none -> 124 us  [local(): pl.pallas_call(kernel, out_shape=jax.ShapeDtypeStruct((OWN, W, 192), F32)...]
    dot_general x84 -> x0, matrix products: 74 us -> none  [the longest x4 30 us: local(): jnp.dot(hidden, full_down, preferred_element_type=jnp.float32)]
    all_gather x2, waiting for transfers between devices: 37.1 us -> 106 us  [the longest x1 54.6 us: local(): down = lax.all_gather(down_weight, 'ch', axis=0, tiled=True)]
    all_to_all x32 -> x0, local copies, waits for them, and re-layouts: 30.6 us -> none  [the longest x12 25.7 us: local(): lax.all_to_all(mixed.reshape(owned.shape), 'ch', split_axis=3, concat_axi...]
    all_to_all x4 -> x0, starting transfers between devices: 23.3 us -> none  [the longest x1 8.63 us: local(): lax.all_to_all(jnp.stack((real_lon, imag_lon)), 'lat', split_axis=3, conc...]
    unnamed x5 -> x0, other arithmetic: 21 us -> none
    all_to_all x4 -> x0, waiting for transfers between devices: 17.9 us -> none  [the longest x1 10.1 us: local(): lax.all_to_all(jnp.stack((real_lon, imag_lon)), 'lat', split_axis=3, conc...]
  transfers between devices with their start and end apart: 6 -> 2, of which waited for: 4 -> 2; matrix products, arithmetic and copies ran while one was open for 5% -> 1% of each run, Pallas kernels for 0% -> 0%
where the time goes in v1:
time: 257 us
  Pallas kernels  124 us (48%)
  waiting for transfers between devices  108 us (42%)
  between operations  13.4 us (5%)
  local copies, waits for them, and re-layouts  10.4 us (4%)
    pallas_call x1, Pallas kernels, local(): pl.pallas_call(kernel, out_shape=jax.ShapeDtypeStruct((OWN, W, 192), F32)...  124 us
    all_gather x1, waiting for transfers between devices, local(): down = lax.all_gather(down_weight, 'ch', axis=0, tiled=True)  54.6 us
    all_gather x1, waiting for transfers between devices, local(): up = lax.all_gather(up_weight, 'ch', axis=1, tiled=True)  51.5 us
    unnamed x17, local copies, waits for them, and re-layouts  7.97 us
  transfers between devices with their start and end apart: 2, of which 2 were waited for; matrix products, arithmetic and copies ran while one was open for 1% of the time, Pallas kernels for 0%

profile of v1, /device:TPU:4, one launch (start us, length us, event | category | flops | bytes accessed | tf_op | source)
XLA Modules:
  0.0 256.7 jit_solution(1311814349416846529)
XLA Ops:
  6.5 0.0 all-gather.3.cloned.1.call-start
  6.5 0.7 all-gather.3.cloned.1.call-update
  7.3 0.0 all-gather.5.cloned.1.call-start
  7.3 0.7 all-gather.5.cloned.1.call-update
  8.0 0.7 reshape.88
  8.7 0.7 convert_element_type.2
  9.4 1.1 copy.18
  10.5 0.7 pad_convert_fusion
  11.2 0.3 scatter.19
  11.5 0.1 scatter.20.small
  11.6 51.5 %all-gather.3.cloned.1.call-done.up = bf16[768,3072]{1,0:T(8,128)(2,1)} async-done(((bf16[768,768]{1,0:T(8,128)(2,1)}), bf16[768,3072]{1,0:T(8,128)(2,1)}) %all-gather.3.cloned.1.call-update) | async-done | bytes 4718608 | tf_op jit(solution)/shard_map/all_gather | solution.py:281
  63.0 54.6 %all-gather.5.cloned.1.call-done.down = bf16[3072,768]{1,0:T(8,128)(2,1)} async-done(((bf16[768,768]{1,0:T(8,128)(2,1)}), bf16[3072,768]{1,0:T(8,128)(2,1)}) %all-gather.5.cloned.1.call-update) | async-done | bytes 4718608 | tf_op jit(solution)/shard_map/all_gather | solution.py:282
  117.7 0.0 copy-start
  117.7 0.9 copy-done
  118.6 0.0 copy-start.1
  118.6 0.9 copy-done.1
  119.5 0.0 copy-start.2
  119.6 0.9 copy-done.2
  120.5 0.0 copy-start.3
  120.5 0.9 copy-done.3
  121.4 0.0 copy-start.4
  121.4 0.9 copy-done.4
  122.3 0.0 copy-start.5
  122.3 0.9 copy-done.5
  123.2 0.0 copy-start.6
  123.2 0.7 copy-done.6
  123.9 0.0 copy-start.7
  123.9 0.7 copy-done.7
  124.6 123.9 %rollout.1 = f32[3,180,192]{2,1,0:T(8,128)S(1)} custom-call(f32[3,180,192]{2,1,0:T(8,128)S(1)} %bitcast.4, f32[8,768]{1,0:T(8,128)S(1)} %scatter.20.small, f32[2,2,96,96]{3,2,1,0:T(8,128)S(1)} %copy-done, f32[2,2,96]{2,1,0:T(2,128)S(1)} %copy-done.6, f32[2,2,96,96]{3,2,1,0:T(8,128)S(1)} %copy-done.1, f32[2,2,96]{2,1,0:T(2,128)S(1)} %copy-done.7, ...), custom_call_target="tpu_custom_call" | custom-call | tf_op jit(solution)/shard_map/rollout/pallas_call | solution.py:291
  248.5 1.4 copy.15
Async XLA Ops:
  6.5 56.5 %all-gather.3.cloned.1.call-start = ((), (), s32[]{:S(2)}) async-start(), calls=%async_computation | async-start | bytes 5898240 | tf_op jit(solution)/shard_map/all_gather | solution.py:281
  7.3 110.4 %all-gather.5.cloned.1.call-start = ((), (), s32[]{:S(2)}) async-start(), calls=%async_computation.1 | async-start | bytes 5898240 | tf_op jit(solution)/shard_map/all_gather | solution.py:282
  117.7 0.9 copy-start
  118.6 0.9 copy-start.1
  119.5 0.9 copy-start.2
  120.5 0.9 copy-start.3
  121.4 0.9 copy-start.4
  122.3 0.9 copy-start.5
  123.2 0.7 copy-start.6
  123.9 0.7 copy-start.7
Sparse Core Ops, SparseCore 0:
  9.0 54.0 all-gather.2
  64.7 52.9 all-gather.4

commit v2 on v1

--- a/solution.py
+++ b/solution.py
@@ -95,8 +95,9 @@
 def kernel(
     state, small, fin, finb, fout, foutb, up, down, fwd, back, t_to, t_fro,
     out,
-    xin, smalls, x, nb, fsend, frecv, bsend, brecv, w1, b1, w2, b2, par, hid, lat_to, lat_fro, n3,
+    xin, smalls, x, nb, fsend, frecv, bsend, brecv, w1, b1, w2, b2, par, hid, lat_to, lat_fro, n3, wts,
     in_s, in_r, sm_s, sm_r, f_s, f_r, b_s, b_r, o_s, o_r,
+    own_r, wa_s, wa_r, wb_s, wb_r, wc_s, wc_r, wd_s, wd_r,
 ):
     l = lax.axis_index("lat")
     c = lax.axis_index("ch")
@@ -126,6 +127,84 @@
         def _(i=i):
             pltpu.make_async_copy(state.at[i], xin.at[i], in_r.at[i]).start()
             pltpu.make_async_copy(small, smalls.at[i], sm_r.at[i]).start()
+
+    k = lax.rem(l, 2)
+    cy = lax.rem(l // 2, 4)
+    cz = l // 8
+    py, pz = lax.rem(cy, 2), lax.rem(cz, 2)
+    mine = 2 * pz + py
+    at_y, at_z, at_d = 2 * pz + 1 - py, 2 * (1 - pz) + py, 2 * (1 - pz) + 1 - py
+    shards = (up, down)
+
+    def chip(dy, dz, core):
+        return (lax.rem(cz + dz + 4, 4) * 4 + lax.rem(cy + dy + 4, 4)) * 2 + core
+
+    def foreign(j):
+        return lax.rem(c + 1 + j, NC)
+
+    def take(sems, *at):
+        ref = wts.at[0, 0, 0, pl.ds(0, 3)]
+        pltpu.make_async_copy(ref, ref, sems.at[at]).wait()
+
+    def pass_on(m, piece, axis, s_sem, r_sem):
+        for j in range(3):
+            for half, sign in ((0, 1), (1, -1)):
+                ref = wts.at[foreign(j), m, k, piece, half]
+                to = chip(sign, 0, k) if axis == 0 else chip(0, sign, k)
+                pltpu.make_async_remote_copy(
+                    ref, ref, s_sem, r_sem, device_id=(to, c), device_id_type=MESH).start()
+
+    def share(m, piece, stage):
+        for j in range(3):
+            ref = wts.at[foreign(j), m, k, piece]
+            pltpu.make_async_remote_copy(
+                ref, ref, wd_s, wd_r.at[stage, m], device_id=(chip(0, 0, 1 - k), c), device_id_type=MESH).start()
+
+    for m in range(2):
+        for i in range(OWN):
+            @pl.when(c != i)
+            def _(m=m, i=i):
+                pltpu.make_async_remote_copy(
+                    shards[m].at[k, mine], wts.at[c, m, k, mine], wa_s.at[m, i], wa_r.at[m],
+                    device_id=(l, i), device_id_type=MESH).start()
+
+    @pl.when(owner)
+    def _():
+        for m in range(2):
+            pltpu.make_async_copy(shards[m], wts.at[c, m], own_r.at[m]).start()
+
+    def weights_1():
+        for m in range(2):
+            take(wa_r, m)
+            pass_on(m, mine, 0, wb_s.at[m, 0], wb_r.at[m, 0])
+            pass_on(m, mine, 1, wb_s.at[m, 1], wb_r.at[m, 1])
+        for m in range(2):
+            share(m, mine, 0)
+
+    def weights_2():
+        take(wb_r, 0, 1)
+        pass_on(0, at_z, 0, wc_s.at[0], wc_r.at[0])
+        take(wb_r, 1, 0)
+        pass_on(1, at_y, 1, wc_s.at[1], wc_r.at[1])
+        take(wb_r, 0, 0)
+        take(wb_r, 1, 1)
+        for m in range(2):
+            share(m, at_y, 1)
+            share(m, at_z, 2)
+
+    def weights_3():
+        for m in range(2):
+            take(wc_r, m)
+            share(m, at_d, 3)
+        ref = wts.at[pl.ds(0, 3), 0]
+        pltpu.make_async_copy(ref, ref, wd_s).wait()
+        for m in range(2):
+            pltpu.make_async_copy(wts.at[c, m], wts.at[c, m], own_r.at[m]).wait()
+            for stage in range(4):
+                take(wd_r, stage, m)
+            for axis in range(2):
+                take(wb_s, m, axis)
+            take(wc_s, m)
 
     for w_ref, b_ref, src, bsrc in ((w1, b1, fin, finb), (w2, b2, fout, foutb)):
         w_ref[...] = jnp.zeros_like(w_ref)
@@ -185,6 +264,7 @@
             lax.fori_loop(1, ND, send, 0)
             pltpu.make_async_copy(
                 fsend.at[2 * c + blk, l // 2], frecv.at[row], f_r).start()
+            pl.when(s == 0)(weights_1)
 
         pltpu.make_async_copy(frecv, frecv, f_r).wait()
         got = frecv[...].reshape(H * 8, 128)
@@ -218,6 +298,7 @@
         @pl.when(owner)
         def _():
             pltpu.make_async_copy(bsend.at[row], brecv.at[2 * c + blk, l // 2], b_r).start()
+            pl.when(s == 0)(weights_2)
             pltpu.make_async_copy(brecv, brecv, b_r).wait()
             packed = jnp.concatenate(
                 [brecv[b].reshape(128, 128)[:, 0:BS].astype(F32) for b in range(NB)], axis=1).astype(BF)
@@ -225,15 +306,18 @@
             v = x[...] + jnp.dot(back[...], packed, preferred_element_type=F32) * SCALE
             x[...] = v
             nb[...] = norm(v, par[1:2, :], par[3:4, :]).astype(BF)
+            pl.when(s == 0)(weights_3)
             for q in range(NC):
                 for j in range(3):
-                    pre = jnp.dot(nb[...], up[:, q * 768 + j * 256:q * 768 + (j + 1) * 256], preferred_element_type=F32)
-                    pre = pre + smalls[q, 5:6, j * 256:(j + 1) * 256]
+                    cols = slice(j * 256, (j + 1) * 256)
+                    weight = wts[q, 0, :, :, :, :, cols].reshape(D, 256)
+                    pre = jnp.dot(nb[...], weight, preferred_element_type=F32) + smalls[q, 5:6, cols]
                     act = 0.5 * pre * (1.0 + lax.erf(pre * math.sqrt(0.5)))
                     hid[:, q * 768 + j * 256:q * 768 + (j + 1) * 256] = act.astype(BF)
             for j in range(3):
                 cols = slice(j * 256, (j + 1) * 256)
-                mixed = jnp.dot(hid[...], down[:, cols], preferred_element_type=F32)
+                weight = wts[:, 1, :, :, :, :, cols].reshape(FF, 256)
+                mixed = jnp.dot(hid[...], weight, preferred_element_type=F32)
                 x[:, cols] = x[:, cols] + mixed + par[4:5, cols]
             pltpu.make_async_copy(fsend.at[0:7], fsend.at[0:7], f_s).wait()
             pltpu.make_async_copy(fsend.at[7, 0:15], fsend.at[7, 0:15], f_s).wait()
@@ -246,6 +330,13 @@
         return carry
 
     lax.fori_loop(0, STEPS, step, 0)
+
+    for m in range(2):
+        for i in range(OWN):
+            @pl.when(c != i)
+            def _(m=m, i=i):
+                ref = shards[m].at[k, mine]
+                pltpu.make_async_copy(ref, ref, wa_s.at[m, i]).wait()
 
     @pl.when(owner)
     def _():
@@ -278,8 +369,8 @@
     state, norm_gains, channel_biases, filter_in, filter_in_bias, filter_out, filter_out_bias,
     up_weight, up_bias, down_weight,
 ):
-    up = lax.all_gather(up_weight, "ch", axis=1, tiled=True)
-    down = lax.all_gather(down_weight, "ch", axis=0, tiled=True)
+    up = up_weight.reshape(2, 4, 2, 48, 768)
+    down = down_weight.reshape(2, 4, 2, 48, 768)
     small = jnp.zeros((8, D), F32)
     small = small.at[0:2, 0:192].set(norm_gains.astype(F32))
     small = small.at[2:5, 0:192].set(channel_biases.astype(F32))
@@ -291,7 +382,7 @@
     result = pl.pallas_call(
         kernel,
         out_shape=jax.ShapeDtypeStruct((OWN, W, 192), F32),
-        in_specs=[anyspace, vm] + [vm] * 10,
+        in_specs=[anyspace] + [vm] * 5 + [anyspace] * 2 + [vm] * 4,
         out_specs=vm,
         scratch_shapes=[
             pltpu.VMEM((NC, W, 192), F32),
@@ -311,8 +402,10 @@
             pltpu.VMEM((2, 768, 768), BF),
             pltpu.VMEM((2, 768, 768), BF),
             pltpu.VMEM((3 * R, D), BF),
+            pltpu.VMEM((NC, 2, 2, 4, 2, 48, 768), BF),
             sem((OWN,)), sem((NC,)), sem((OWN,)), sem((NC,)),
             sem, sem, sem, sem, sem((NC,)), sem((OWN,)),
+            sem((2,)), sem((2, OWN)), sem((2,)), sem((2, 2)), sem((2, 2)), sem((2,)), sem((2,)), sem, sem((4, 2)),
         ],
         compiler_params=pltpu.CompilerParams(
             has_side_effects=True, vmem_limit_bytes=50 * 1024 * 1024),

time: 257 us -> 145 us (0.56)
  waiting for transfers between devices: 108 us -> 0 us
  between operations: 13.4 us -> 0.12 us
  Pallas kernels: 124 us -> 137 us
  local copies, waits for them, and re-layouts: 10.4 us -> 6.29 us
    all_gather x2 -> x0, waiting for transfers between devices: 106 us -> none  [the longest x1 54.6 us: local(): down = lax.all_gather(down_weight, 'ch', axis=0, tiled=True)]
    pallas_call x1, Pallas kernels: 124 us -> 137 us  [local(): pl.pallas_call(kernel, out_shape=jax.ShapeDtypeStruct((OWN, W, 192), F32)...]
    unnamed x17 -> x19, local copies, waits for them, and re-layouts: 7.97 us -> 3.75 us
  transfers between devices with their start and end apart: 2 -> 0, of which waited for: 2 -> 0; matrix products, arithmetic and copies ran while one was open for 1% -> 0% of each run, Pallas kernels for 0% -> 0%
where the time goes in v2:
time: 145 us
  Pallas kernels  137 us (94%)
  local copies, waits for them, and re-layouts  6.29 us (4%)
    pallas_call x1, Pallas kernels, local(): pl.pallas_call(kernel, out_shape=jax.ShapeDtypeStruct((OWN, W, 192), F32)...  137 us
    unnamed x19, local copies, waits for them, and re-layouts  3.75 us

profile of v2, /device:TPU:4, one launch (start us, length us, event | category | flops | bytes accessed | tf_op | source)
XLA Modules:
  0.0 145.0 jit_solution(9741776079180191203)
XLA Ops:
  0.0 0.0 copy-start.3
  0.0 0.0 copy-start.4
  0.0 0.0 copy-start.6
  0.0 0.0 copy-start.5
  0.0 0.0 copy-start.2
  0.0 0.0 copy-start.1
  0.0 0.8 reshape.96
  0.8 0.7 convert_element_type.2
  1.5 0.7 pad_convert_fusion
  2.2 0.3 scatter.19
  2.5 0.1 scatter.20.small
  2.6 1.1 copy.18
  3.7 0.0 copy-done.3
  3.7 0.0 copy-done.4
  3.7 0.0 copy-done.6
  3.7 0.0 copy-done.5
  3.7 0.0 copy-done.2
  3.8 0.0 copy-done.1
  3.8 0.0 copy-start
  3.8 1.3 copy-done
  5.0 0.0 copy-start.7
  5.0 0.7 copy-done.7
  5.7 0.0 copy-start.8
  5.7 0.7 copy-done.8
  6.4 137.2 %rollout.1 = f32[3,180,192]{2,1,0:T(8,128)S(1)} custom-call(f32[3,180,192]{2,1,0:T(8,128)S(1)} %bitcast.7, f32[8,768]{1,0:T(8,128)S(1)} %scatter.20.small, f32[2,2,96,96]{3,2,1,0:T(8,128)S(1)} %copy-done.1, f32[2,2,96]{2,1,0:T(2,128)S(1)} %copy-done.7, f32[2,2,96,96]{3,2,1,0:T(8,128)S(1)} %copy-done.2, f32[2,2,96]{2,1,0:T(2,128)S(1)} %copy-done.8, ...), custom_call_target="tpu_custom_call" | custom-call | tf_op jit(solution)/shard_map/rollout/pallas_call | solution.py:382
  143.6 1.4 copy.15
Async XLA Ops:
  0.0 3.7 %copy-start.3 = (bf16[2,192,192]{2,1,0:T(8,128)(2,1)S(1)}, bf16[2,192,192]{2,1,0:T(8,128)(2,1)}, u32[]{:S(2)}) copy-start(bf16[2,192,192]{2,1,0:T(8,128)(2,1)} %constant.96.clone.t_fro) | copy-start | bytes 442372
  0.0 3.7 %copy-start.4 = (bf16[2,192,192]{2,1,0:T(8,128)(2,1)S(1)}, bf16[2,192,192]{2,1,0:T(8,128)(2,1)}, u32[]{:S(2)}) copy-start(bf16[2,192,192]{2,1,0:T(8,128)(2,1)} %constant.95.clone.t_to) | copy-start | bytes 442372
  0.0 3.7 %copy-start.6 = (bf16[192,256]{1,0:T(8,128)(2,1)S(1)}, bf16[192,256]{1,0:T(8,128)(2,1)}, u32[]{:S(2)}) copy-start(bf16[192,256]{1,0:T(8,128)(2,1)} %constant.94.clone.back) | copy-start | bytes 294916
  0.0 3.7 %copy-start.5 = (bf16[128,576]{1,0:T(8,128)(2,1)S(1)}, bf16[128,576]{1,0:T(8,128)(2,1)}, u32[]{:S(2)}) copy-start(bf16[128,576]{1,0:T(8,128)(2,1)} %constant.93.clone.fwd) | copy-start | bytes 442372
  0.0 3.7 %copy-start.2 = (f32[2,2,96,96]{3,2,1,0:T(8,128)S(1)}, f32[2,2,96,96]{3,2,1,0:T(8,128)}, u32[]{:S(2)}) copy-start(f32[2,2,96,96]{3,2,1,0:T(8,128)} %fout.1) | copy-start | bytes 442372
  0.0 3.7 %copy-start.1 = (f32[2,2,96,96]{3,2,1,0:T(8,128)S(1)}, f32[2,2,96,96]{3,2,1,0:T(8,128)}, u32[]{:S(2)}) copy-start(f32[2,2,96,96]{3,2,1,0:T(8,128)} %fin.1) | copy-start | bytes 442372
  3.8 1.3 copy-start
  5.0 0.7 copy-start.7
  5.7 0.7 copy-start.8

commit v3 on v1

--- a/solution.py
+++ b/solution.py
@@ -95,8 +95,9 @@
 def kernel(
     state, small, fin, finb, fout, foutb, up, down, fwd, back, t_to, t_fro,
     out,
-    xin, smalls, x, nb, fsend, frecv, bsend, brecv, w1, b1, w2, b2, par, hid, lat_to, lat_fro, n3,
+    xin, smalls, x, nb, fsend, frecv, bsend, brecv, w1, b1, w2, b2, par, hid, lat_to, lat_fro, n3, wts, tall, stat, stats,
     in_s, in_r, sm_s, sm_r, f_s, f_r, b_s, b_r, o_s, o_r,
+    own_r, wa_s, wa_r, wb_s, wb_r, wc_s, wc_r, wd_s, wd_r, st_s, st_r,
 ):
     l = lax.axis_index("lat")
     c = lax.axis_index("ch")
@@ -104,6 +105,15 @@
     row = l * OWN + c
     blk = lax.rem(l, 2)
     owner = c < OWN
+
+    barrier = pltpu.get_barrier_semaphore()
+
+    def greet(i, carry):
+        d = lax.rem(me + i, ND)
+        pl.semaphore_signal(barrier, inc=1, device_id=(d // NC, lax.rem(d, NC)), device_id_type=MESH)
+        return carry
+
+    lax.fori_loop(1, ND, greet, 0)
 
     def to_owner(i):
         return (
@@ -115,17 +125,59 @@
                 device_id=(l, i), device_id_type=MESH),
         )
 
-    for i in range(OWN):
-        @pl.when(c != i)
-        def _(i=i):
-            a, b = to_owner(i)
-            a.start()
-            b.start()
-
-        @pl.when(c == i)
-        def _(i=i):
-            pltpu.make_async_copy(state.at[i], xin.at[i], in_r.at[i]).start()
-            pltpu.make_async_copy(small, smalls.at[i], sm_r.at[i]).start()
+    k = lax.rem(l, 2)
+    cy = lax.rem(l // 2, 4)
+    cz = l // 8
+    py, pz = lax.rem(cy, 2), lax.rem(cz, 2)
+    mine = 2 * pz + py
+    at_y, at_z, at_d = 2 * pz + 1 - py, 2 * (1 - pz) + py, 2 * (1 - pz) + 1 - py
+    shards = (up, down)
+
+    def chip(dy, dz, core):
+        return (lax.rem(cz + dz + 4, 4) * 4 + lax.rem(cy + dy + 4, 4)) * 2 + core
+
+    def foreign(j):
+        return lax.rem(c + 1 + j, NC)
+
+    def take(sems, *at):
+        ref = wts.at[0, 0, 0, pl.ds(0, 3)]
+        pltpu.make_async_copy(ref, ref, sems.at[at]).wait()
+
+    def pass_on(m, piece, axis, s_sem, r_sem):
+        for j in range(3):
+            for half, sign in ((0, 1), (1, -1)):
+                ref = wts.at[foreign(j), m, k, piece, half]
+                to = chip(sign, 0, k) if axis == 0 else chip(0, sign, k)
+                pltpu.make_async_remote_copy(
+                    ref, ref, s_sem, r_sem, device_id=(to, c), device_id_type=MESH).start()
+
+    def share(m, piece, stage):
+        for j in range(3):
+            ref = wts.at[foreign(j), m, k, piece]
+            pltpu.make_async_remote_copy(
+                ref, ref, wd_s, wd_r.at[stage, m], device_id=(chip(0, 0, 1 - k), c), device_id_type=MESH).start()
+
+    def weights_1(m):
+        take(wa_r, m)
+        pass_on(m, mine, 0, wb_s.at[m, 0], wb_r.at[m, 0])
+        pass_on(m, mine, 1, wb_s.at[m, 1], wb_r.at[m, 1])
+        share(m, mine, 0)
+
+    def weights_2(m):
+        take(wb_r, m, 1 - m)
+        pass_on(m, (at_z, at_y)[m], m, wc_s.at[m], wc_r.at[m])
+        take(wb_r, m, m)
+        share(m, at_y, 1)
+        share(m, at_z, 2)
+
+    def weights_3(m):
+        take(wc_r, m)
+        share(m, at_d, 3)
+
+    def weights_4(m):
+        pltpu.make_async_copy(wts.at[c, m], wts.at[c, m], own_r.at[m]).wait()
+        for stage in range(4):
+            take(wd_r, stage, m)
 
     for w_ref, b_ref, src, bsrc in ((w1, b1, fin, finb), (w2, b2, fout, foutb)):
         w_ref[...] = jnp.zeros_like(w_ref)
@@ -142,50 +194,119 @@
     spread_out(t_to, lat_to)
     spread_out(t_fro, lat_fro)
 
+    fsend[...] = jnp.zeros_like(fsend)
+    n3[...] = jnp.zeros_like(n3)
+    tall[...] = jnp.zeros_like(tall)
+    lane = lax.broadcasted_iota(jnp.int32, (W, 128), 1)
+    for r in range(OWN):
+        v = state[r]
+        total = jnp.sum(v, -1, keepdims=True)
+        squares = jnp.sum(v * v, -1, keepdims=True)
+        tall[r * R:r * R + W, :] = jnp.where(lane == 0, total, jnp.where(lane == 1, squares, 0.0))
+    stat[...] = tall[...].T[0:8, :]
+
     @pl.when(owner)
     def _():
+        for m in range(2):
+            pltpu.make_async_copy(shards[m], wts.at[c, m], own_r.at[m]).start()
+
+    pl.semaphore_wait(barrier, ND - 1)
+    for j in range(NC):
+        @pl.when(c != j)
+        def _(j=j):
+            pltpu.make_async_remote_copy(
+                stat, stats.at[c], st_s.at[j], st_r.at[c], device_id=(l, j), device_id_type=MESH).start()
+
+        @pl.when(c == j)
+        def _(j=j):
+            pltpu.make_async_copy(stat, stats.at[j], st_r.at[j]).start()
+
+    for m in range(2):
+        for i in range(OWN):
+            @pl.when(c != i)
+            def _(m=m, i=i):
+                pltpu.make_async_remote_copy(
+                    shards[m].at[k, mine], wts.at[c, m, k, mine], wa_s.at[m, i], wa_r.at[m],
+                    device_id=(l, i), device_id_type=MESH).start()
+
+    for i in range(OWN):
+        @pl.when(c != i)
+        def _(i=i):
+            a, b = to_owner(i)
+            a.start()
+            b.start()
+
+        @pl.when(c == i)
+        def _(i=i):
+            pltpu.make_async_copy(state.at[i], xin.at[i], in_r.at[i]).start()
+            pltpu.make_async_copy(small, smalls.at[i], sm_r.at[i]).start()
+
+    for j in range(NC):
+        pltpu.make_async_copy(stats.at[j], stats.at[j], st_r.at[j]).wait()
+    total = (stats[0] + stats[1]) + (stats[2] + stats[3])
+    mean = total[0:1] / D
+    spread = lax.rsqrt(total[1:2] / D - mean * mean + EPS)
+    line = lax.broadcasted_iota(jnp.int32, (128, 640), 0)
+    tall[...] = jnp.where(line == 0, mean, jnp.where(line == 1, spread, 0.0)).T
+    for r in range(OWN):
+        at = slice(r * R, r * R + W)
+        n = (state[r] - tall[at, 0:1]) * tall[at, 1:2] * small[0:1, 0:192] + small[2:3, 0:192]
+        hi, lo = parts(n)
+        n3[0:W, 0:192] = hi
+        n3[R:R + W, 0:192] = hi
+        n3[2 * R:2 * R + W, 0:192] = lo
+        lon = jnp.dot(fwd[...], n3[:, 0:192], preferred_element_type=F32)
+        for j in range(2):
+            fsend[2 * r + j, :, :, 0:BS] = lon[:, j * BS:(j + 1) * BS].reshape(G, 8, BS).astype(BF)
+
+    def send_first(i, carry):
+        dl = lax.rem(l + i, NL)
+        for r in range(OWN):
+            pltpu.make_async_remote_copy(
+                fsend.at[2 * r + lax.rem(dl, 2), dl // 2], frecv.at[l * OWN + r], f_s, f_r,
+                device_id=(dl, c), device_id_type=MESH).start()
+        return carry
+
+    lax.fori_loop(1, NL, send_first, 0)
+    for r in range(OWN):
+        pltpu.make_async_copy(fsend.at[2 * r + blk, l // 2], frecv.at[l * OWN + r], f_r).start()
+    pl.when(owner)(lambda: weights_1(0))
+
+    def own_row():
         for j in range(NC):
             pltpu.make_async_copy(xin.at[j], xin.at[j], in_r.at[j]).wait()
             pltpu.make_async_copy(smalls.at[j], smalls.at[j], sm_r.at[j]).wait()
         par[0:5, :] = jnp.concatenate([smalls[j, 0:5, 0:192] for j in range(NC)], axis=1)
-        x[0:W, :] = jnp.concatenate([xin[j] for j in range(NC)], axis=1)
+        v = jnp.concatenate([xin[j] for j in range(NC)], axis=1)
+        x[0:W, :] = v + norm(v, par[0:1, :], par[2:3, :])
         x[W:R, :] = jnp.zeros((R - W, D), F32)
-        fsend[...] = jnp.zeros_like(fsend)
-
-    for i in range(OWN):
-        @pl.when(c != i)
-        def _(i=i):
-            a, b = to_owner(i)
-            a.wait_send()
-            b.wait_send()
+
+    def send_row():
+        v = x[...]
+        n = norm(v, par[0:1, :], par[2:3, :])
+        x[...] = v + n
+        hi, lo = parts(n)
+        n3[0:R, :] = hi
+        n3[R:2 * R, :] = hi
+        n3[2 * R:3 * R, :] = lo
+        lon = jnp.dot(fwd[...], n3[...], preferred_element_type=F32)
+        for b in range(NB):
+            fsend[b, :, :, 0:BS] = lon[:, b * BS:(b + 1) * BS].reshape(G, 8, BS).astype(BF)
+
+        def send(i, carry):
+            d = lax.rem(me + i, ND)
+            dl, dc = d // NC, lax.rem(d, NC)
+            src = fsend.at[2 * dc + lax.rem(dl, 2), dl // 2]
+
+            pltpu.make_async_remote_copy(
+                src, frecv.at[row], f_s, f_r, device_id=(dl, dc), device_id_type=MESH).start()
+            return carry
+
+        lax.fori_loop(1, ND, send, 0)
+        pltpu.make_async_copy(
+            fsend.at[2 * c + blk, l // 2], frecv.at[row], f_r).start()
 
     def step(s, carry):
-        @pl.when(owner)
-        def _():
-            v = x[...]
-            n = norm(v, par[0:1, :], par[2:3, :])
-            x[...] = v + n
-            hi, lo = parts(n)
-            n3[0:R, :] = hi
-            n3[R:2 * R, :] = hi
-            n3[2 * R:3 * R, :] = lo
-            lon = jnp.dot(fwd[...], n3[...], preferred_element_type=F32)
-            for b in range(NB):
-                fsend[b, :, :, 0:BS] = lon[:, b * BS:(b + 1) * BS].reshape(G, 8, BS).astype(BF)
-
-            def send(i, carry):
-                d = lax.rem(me + i, ND)
-                dl, dc = d // NC, lax.rem(d, NC)
-                src = fsend.at[2 * dc + lax.rem(dl, 2), dl // 2]
-
-                pltpu.make_async_remote_copy(
-                    src, frecv.at[row], f_s, f_r, device_id=(dl, dc), device_id_type=MESH).start()
-                return carry
-
-            lax.fori_loop(1, ND, send, 0)
-            pltpu.make_async_copy(
-                fsend.at[2 * c + blk, l // 2], frecv.at[row], f_r).start()
-
         pltpu.make_async_copy(frecv, frecv, f_r).wait()
         got = frecv[...].reshape(H * 8, 128)
         spec = jnp.dot(lat_to[0], got, preferred_element_type=F32)
@@ -218,34 +339,104 @@
         @pl.when(owner)
         def _():
             pltpu.make_async_copy(bsend.at[row], brecv.at[2 * c + blk, l // 2], b_r).start()
+
+            @pl.when(s == 0)
+            def _():
+                weights_1(1)
+                weights_2(0)
+                own_row()
+                weights_3(0)
+
             pltpu.make_async_copy(brecv, brecv, b_r).wait()
+
+            @pl.when(s == 0)
+            def _():
+                weights_2(1)
+
             packed = jnp.concatenate(
                 [brecv[b].reshape(128, 128)[:, 0:BS].astype(F32) for b in range(NB)], axis=1).astype(BF)
             packed = jnp.concatenate([packed, packed], axis=0)
             v = x[...] + jnp.dot(back[...], packed, preferred_element_type=F32) * SCALE
             x[...] = v
             nb[...] = norm(v, par[1:2, :], par[3:4, :]).astype(BF)
+
+            @pl.when(s == 0)
+            def _():
+                weights_4(0)
+
             for q in range(NC):
                 for j in range(3):
-                    pre = jnp.dot(nb[...], up[:, q * 768 + j * 256:q * 768 + (j + 1) * 256], preferred_element_type=F32)
-                    pre = pre + smalls[q, 5:6, j * 256:(j + 1) * 256]
+                    cols = slice(j * 256, (j + 1) * 256)
+                    weight = wts[q, 0, :, :, :, :, cols].reshape(D, 256)
+                    pre = jnp.dot(nb[...], weight, preferred_element_type=F32) + smalls[q, 5:6, cols]
                     act = 0.5 * pre * (1.0 + lax.erf(pre * math.sqrt(0.5)))
                     hid[:, q * 768 + j * 256:q * 768 + (j + 1) * 256] = act.astype(BF)
+
+            @pl.when(s == 0)
+            def _():
+                weights_3(1)
+                weights_4(1)
+
             for j in range(3):
                 cols = slice(j * 256, (j + 1) * 256)
-                mixed = jnp.dot(hid[...], down[:, cols], preferred_element_type=F32)
+                weight = wts[:, 1, :, :, :, :, cols].reshape(FF, 256)
+                mixed = jnp.dot(hid[...], weight, preferred_element_type=F32)
                 x[:, cols] = x[:, cols] + mixed + par[4:5, cols]
+
+            @pl.when(s < STEPS - 1)
+            def _():
+                sent_f(s)
+                send_row()
+
+            pltpu.make_async_copy(bsend.at[0:95], bsend.at[0:95], b_s).wait()
+
+        @pl.when(jnp.logical_not(owner))
+        def _():
+            pl.when(s == 0)(lambda: sent_f(s))
+            pltpu.make_async_copy(bsend, bsend, b_s).wait()
+
+        return carry
+
+    def sent_f(s):
+        @pl.when(s == 0)
+        def _():
+            pltpu.make_async_copy(bsend.at[0:93], bsend.at[0:93], f_s).wait()
+
+        @pl.when(s > 0)
+        def _():
             pltpu.make_async_copy(fsend.at[0:7], fsend.at[0:7], f_s).wait()
             pltpu.make_async_copy(fsend.at[7, 0:15], fsend.at[7, 0:15], f_s).wait()
-            pltpu.make_async_copy(bsend.at[0:95], bsend.at[0:95], b_s).wait()
-
-        @pl.when(jnp.logical_not(owner))
-        def _():
-            pltpu.make_async_copy(bsend, bsend, b_s).wait()
-
-        return carry
 
     lax.fori_loop(0, STEPS, step, 0)
+
+    @pl.when(owner)
+    def _():
+        sent_f(1)
+        ref = wts.at[pl.ds(0, 3), 0]
+        pltpu.make_async_copy(ref, ref, wd_s).wait()
+        for m in range(2):
+            for axis in range(2):
+                take(wb_s, m, axis)
+            take(wc_s, m)
+
+    for i in range(OWN):
+        @pl.when(c != i)
+        def _(i=i):
+            a, b = to_owner(i)
+            a.wait_send()
+            b.wait_send()
+
+    for j in range(NC):
+        @pl.when(c != j)
+        def _(j=j):
+            pltpu.make_async_copy(stat, stat, st_s.at[j]).wait()
+
+    for m in range(2):
+        for i in range(OWN):
+            @pl.when(c != i)
+            def _(m=m, i=i):
+                ref = shards[m].at[k, mine]
+                pltpu.make_async_copy(ref, ref, wa_s.at[m, i]).wait()
 
     @pl.when(owner)
     def _():
@@ -278,8 +469,8 @@
     state, norm_gains, channel_biases, filter_in, filter_in_bias, filter_out, filter_out_bias,
     up_weight, up_bias, down_weight,
 ):
-    up = lax.all_gather(up_weight, "ch", axis=1, tiled=True)
-    down = lax.all_gather(down_weight, "ch", axis=0, tiled=True)
+    up = up_weight.reshape(2, 4, 2, 48, 768)
+    down = down_weight.reshape(2, 4, 2, 48, 768)
     small = jnp.zeros((8, D), F32)
     small = small.at[0:2, 0:192].set(norm_gains.astype(F32))
     small = small.at[2:5, 0:192].set(channel_biases.astype(F32))
@@ -291,7 +482,7 @@
     result = pl.pallas_call(
         kernel,
         out_shape=jax.ShapeDtypeStruct((OWN, W, 192), F32),
-        in_specs=[anyspace, vm] + [vm] * 10,
+        in_specs=[vm] + [vm] * 5 + [anyspace] * 2 + [vm] * 4,
         out_specs=vm,
         scratch_shapes=[
             pltpu.VMEM((NC, W, 192), F32),
@@ -311,11 +502,16 @@
             pltpu.VMEM((2, 768, 768), BF),
             pltpu.VMEM((2, 768, 768), BF),
             pltpu.VMEM((3 * R, D), BF),
+            pltpu.VMEM((NC, 2, 2, 4, 2, 48, 768), BF),
+            pltpu.VMEM((640, 128), F32),
+            pltpu.VMEM((8, 640), F32),
+            pltpu.VMEM((NC, 8, 640), F32),
             sem((OWN,)), sem((NC,)), sem((OWN,)), sem((NC,)),
             sem, sem, sem, sem, sem((NC,)), sem((OWN,)),
+            sem((2,)), sem((2, OWN)), sem((2,)), sem((2, 2)), sem((2, 2)), sem((2,)), sem((2,)), sem, sem((4, 2)), sem((NC,)), sem((NC,)),
         ],
         compiler_params=pltpu.CompilerParams(
-            has_side_effects=True, vmem_limit_bytes=50 * 1024 * 1024),
+            collective_id=0, has_side_effects=True, vmem_limit_bytes=50 * 1024 * 1024),
         name="rollout",
     )(
         state[0], small, filter_in, filter_in_bias, filter_out, filter_out_bias,

time: 257 us -> 142 us (0.55)
  waiting for transfers between devices: 108 us -> 0 us
  between operations: 13.4 us -> 0.12 us
  Pallas kernels: 124 us -> 134 us
  local copies, waits for them, and re-layouts: 10.4 us -> 6.29 us
    all_gather x2 -> x0, waiting for transfers between devices: 106 us -> none  [the longest x1 54.6 us: local(): down = lax.all_gather(down_weight, 'ch', axis=0, tiled=True)]
    pallas_call x1, Pallas kernels: 124 us -> 134 us  [local(): pl.pallas_call(kernel, out_shape=jax.ShapeDtypeStruct((OWN, W, 192), F32)...]
    unnamed x17 -> x19, local copies, waits for them, and re-layouts: 7.97 us -> 3.75 us
  transfers between devices with their start and end apart: 2 -> 0, of which waited for: 2 -> 0; matrix products, arithmetic and copies ran while one was open for 1% -> 0% of each run, Pallas kernels for 0% -> 0%
where the time goes in v3:
time: 142 us
  Pallas kernels  134 us (94%)
  local copies, waits for them, and re-layouts  6.29 us (4%)
    pallas_call x1, Pallas kernels, local(): pl.pallas_call(kernel, out_shape=jax.ShapeDtypeStruct((OWN, W, 192), F32)...  134 us
    unnamed x19, local copies, waits for them, and re-layouts  3.75 us

profile of v3, /device:TPU:4, one launch (start us, length us, event | category | flops | bytes accessed | tf_op | source)
XLA Modules:
  0.0 142.2 jit_solution(3251259702952029018)
XLA Ops:
  0.0 0.0 copy-start.3
  0.0 0.0 copy-start.4
  0.0 0.0 copy-start.6
  0.0 0.0 copy-start.5
  0.0 0.0 copy-start.2
  0.0 0.0 copy-start.1
  0.0 0.8 reshape.96
  0.8 0.7 convert_element_type.2
  1.5 0.7 pad_convert_fusion
  2.2 0.3 scatter.19
  2.5 0.1 scatter.20.small
  2.6 1.1 copy.18
  3.7 0.0 copy-done.3
  3.7 0.0 copy-done.4
  3.7 0.0 copy-done.6
  3.7 0.0 copy-done.5
  3.7 0.0 copy-done.2
  3.8 0.0 copy-done.1
  3.8 0.0 copy-start
  3.8 1.3 copy-done
  5.0 0.0 copy-start.7
  5.0 0.7 copy-done.7
  5.7 0.0 copy-start.8
  5.7 0.7 copy-done.8
  6.4 134.4 %rollout.1 = f32[3,180,192]{2,1,0:T(8,128)S(1)} custom-call(f32[3,180,192]{2,1,0:T(8,128)S(1)} %bitcast.7, f32[8,768]{1,0:T(8,128)S(1)} %scatter.20.small, f32[2,2,96,96]{3,2,1,0:T(8,128)S(1)} %copy-done.1, f32[2,2,96]{2,1,0:T(2,128)S(1)} %copy-done.7, f32[2,2,96,96]{3,2,1,0:T(8,128)S(1)} %copy-done.2, f32[2,2,96]{2,1,0:T(2,128)S(1)} %copy-done.8, ...), custom_call_target="tpu_custom_call" | custom-call | tf_op jit(solution)/shard_map/rollout/pallas_call | solution.py:482
  140.8 1.4 copy.15
Async XLA Ops:
  0.0 3.7 %copy-start.3 = (bf16[2,192,192]{2,1,0:T(8,128)(2,1)S(1)}, bf16[2,192,192]{2,1,0:T(8,128)(2,1)}, u32[]{:S(2)}) copy-start(bf16[2,192,192]{2,1,0:T(8,128)(2,1)} %constant.96.clone.t_fro) | copy-start | bytes 442372
  0.0 3.7 %copy-start.4 = (bf16[2,192,192]{2,1,0:T(8,128)(2,1)S(1)}, bf16[2,192,192]{2,1,0:T(8,128)(2,1)}, u32[]{:S(2)}) copy-start(bf16[2,192,192]{2,1,0:T(8,128)(2,1)} %constant.95.clone.t_to) | copy-start | bytes 442372
  0.0 3.7 %copy-start.6 = (bf16[192,256]{1,0:T(8,128)(2,1)S(1)}, bf16[192,256]{1,0:T(8,128)(2,1)}, u32[]{:S(2)}) copy-start(bf16[192,256]{1,0:T(8,128)(2,1)} %constant.94.clone.back) | copy-start | bytes 294916
  0.0 3.7 %copy-start.5 = (bf16[128,576]{1,0:T(8,128)(2,1)S(1)}, bf16[128,576]{1,0:T(8,128)(2,1)}, u32[]{:S(2)}) copy-start(bf16[128,576]{1,0:T(8,128)(2,1)} %constant.93.clone.fwd) | copy-start | bytes 442372
  0.0 3.7 %copy-start.2 = (f32[2,2,96,96]{3,2,1,0:T(8,128)S(1)}, f32[2,2,96,96]{3,2,1,0:T(8,128)}, u32[]{:S(2)}) copy-start(f32[2,2,96,96]{3,2,1,0:T(8,128)} %fout.1) | copy-start | bytes 442372
  0.0 3.7 %copy-start.1 = (f32[2,2,96,96]{3,2,1,0:T(8,128)S(1)}, f32[2,2,96,96]{3,2,1,0:T(8,128)}, u32[]{:S(2)}) copy-start(f32[2,2,96,96]{3,2,1,0:T(8,128)} %fin.1) | copy-start | bytes 442372
  3.8 1.3 copy-start
  5.0 0.7 copy-start.7
  5.7 0.7 copy-start.8

commit v4 on v3

v4 whole, which is shorter than its diff:
```python
import itertools
import math

import jax
import jax.numpy as jnp
import numpy as np
from jax import lax
from jax.experimental import pallas as pl
from jax.experimental.pallas import tpu as pltpu
from jax.sharding import PartitionSpec as P

D = 768
FF = 3072
W = 180
R = 192
H = 96
M = 64
NB = 8
BS = 96
STEPS = 4
NL = 32
NC = 4
ND = NL * NC
OWN = 3
G = 16
SCALE = 1.0 / math.sqrt(H * W)
EPS = 1e-05
SHRINK = 0.01
HOPS = (0, 1, 2, 1)
OTHERS = sorted(
    (o for o in itertools.product(range(4), range(4), range(4), range(2)) if any(o)),
    key=lambda o: -(HOPS[o[0]] + HOPS[o[1]] + HOPS[o[2]] + 0.3 * o[3]),
)
MESH = pl.DeviceIdType.MESH
BF = jnp.bfloat16
F32 = jnp.float32


def tables():
    modes = np.arange(M)
    w = np.arange(W)
    ang = 2.0 * np.pi / W * ((w[:, None] * modes[None, :]) % W)
    c, s = np.cos(ang), np.sin(ang)
    dbl = np.where(modes == 0, 1.0, 2.0)
    fwd = np.zeros((G, 2, 4, R))
    fwd[:, 0, :, :W] = c.T.reshape(G, 4, W)
    fwd[:, 1, :, :W] = -s.T.reshape(G, 4, W)
    back = np.zeros((R, G, 2, 4))
    back[:W, :, 0, :] = (c * dbl).reshape(W, G, 4)
    back[:W, :, 1, :] = -(s * dbl).reshape(W, G, 4)
    h = np.arange(H)
    ang = 2.0 * np.pi / H * ((h[:, None] * h[None, :]) % H)
    c, s = np.cos(ang), np.sin(ang)
    to = np.block([[c, s], [-s, c]])
    fro = to.T
    fwd, back = halves(fwd.reshape(128, R)), halves(back.reshape(R, 128))
    return (
        np.concatenate([fwd[0], fwd[1], fwd[0]], axis=1),
        np.concatenate(back, axis=1),
        np.concatenate(halves(to), axis=1),
        np.concatenate([halves(fro)[0], halves(fro)[1], halves(fro)[0]], axis=1),
    )


def halves(a):
    a = np.asarray(a, np.float32)
    hi = a.astype(BF)
    return hi, (a - hi.astype(np.float32)).astype(BF)


def parts(v):
    hi = v.astype(BF)
    return hi, (v - hi.astype(F32)).astype(BF)


def norm(v, gain, shift):
    mean = jnp.sum(v, -1, keepdims=True) / D
    spread = jnp.sum(v * v, -1, keepdims=True) / D - mean * mean
    return (v - mean) * lax.rsqrt(spread + EPS) * gain + shift


def kernel(
    state_h, gains_h, biases_h, fin_h, finb_h, fout_h, foutb_h, up, upb_h, down, fwd_h, back_h, to_h, fro_h,
    out,
    state, gains, biases, fin, finb, fout, foutb, upb, fwd, back, t_to, t_fro, small, h_s,
    xin, smalls, x, nb, fsend, frecv, bsend, brecv, w1, b1, w2, b2, par, hid, g32, n3, wts, tall, stat, stats,
    in_s, in_r, sm_s, sm_r, f_s, f_r, b_s, b_r, o_s, o_r,
    own_r, wa_s, wa_r, wb_s, wb_r, wc_s, wc_r, wd_s, wd_r, st_s, st_r,
):
    l = lax.axis_index("lat")
    c = lax.axis_index("ch")
    me = l * NC + c
    row = l * OWN + c
    blk = lax.rem(l, 2)
    owner = c < OWN

    k = lax.rem(l, 2)
    cy = lax.rem(l // 2, 4)
    cz = l // 8
    xs = [lax.rem(c + i, 4) for i in range(4)]
    groups = [[lax.rem(cz + i, 4) * 4 + lax.rem(cy + j, 4) for j in range(4)] for i in range(4)]
    cores = (k, 1 - k)

    fetches = [
        pltpu.make_async_copy(src, dst, h_s.at[i])
        for i, (src, dst) in enumerate((
            (to_h, t_to), (fro_h, t_fro), (fin_h, fin), (fout_h, fout), (finb_h, finb), (foutb_h, foutb),
            (gains_h, gains), (biases_h, biases), (upb_h, upb), (fwd_h, fwd), (back_h, back), (state_h, state)))
    ]
    for fetch in fetches:
        fetch.start()

    barrier = pltpu.get_barrier_semaphore()
    for dx, dy, dz, dk in OTHERS:
        pl.semaphore_signal(
            barrier, inc=1, device_id=(groups[dz][dy] * 2 + cores[dk], xs[dx]), device_id_type=MESH)

    def to_owner(i):
        return (
            pltpu.make_async_remote_copy(
                state.at[i], xin.at[c], in_s.at[i], in_r.at[c],
                device_id=(l, i), device_id_type=MESH),
            pltpu.make_async_remote_copy(
                small, smalls.at[c], sm_s.at[i], sm_r.at[c],
                device_id=(l, i), device_id_type=MESH),
        )

    py, pz = lax.rem(cy, 2), lax.rem(cz, 2)
    mine = 2 * pz + py
    at_y, at_z, at_d = 2 * pz + 1 - py, 2 * (1 - pz) + py, 2 * (1 - pz) + 1 - py
    shards = (up, down)

    def foreign(j):
        return lax.rem(c + 1 + j, NC)

    three = wts.at[0, 0, 0, pl.ds(0, 3)]

    def take(sems, *at):
        pltpu.make_async_copy(three, three, sems.at[at]).wait()

    def pass_on(m, piece, axis, s_sem, r_sem):
        for j in range(3):
            for half, sign in ((0, 1), (1, 3)):
                ref = wts.at[foreign(j), m, k, piece, half]
                to = groups[(0, sign)[axis]][(sign, 0)[axis]] * 2 + k
                pltpu.make_async_remote_copy(
                    ref, ref, s_sem, r_sem, device_id=(to, c), device_id_type=MESH).start()

    def share(m, piece, stage):
        for j in range(3):
            ref = wts.at[foreign(j), m, k, piece]
            pltpu.make_async_remote_copy(
                ref, ref, wd_s, wd_r.at[stage, m], device_id=(groups[0][0] * 2 + 1 - k, c), device_id_type=MESH).start()

    def weights_0(m):
        for i in range(OWN):
            @pl.when(c != i)
            def _(i=i):
                pltpu.make_async_remote_copy(
                    shards[m].at[k, mine], wts.at[c, m, k, mine], wa_s.at[m, i], wa_r.at[m],
                    device_id=(l, i), device_id_type=MESH).start()

    def sent_weights(m):
        for i in range(OWN):
            @pl.when(c != i)
            def _(i=i):
                ref = shards[m].at[k, mine]
                pltpu.make_async_copy(ref, ref, wa_s.at[m, i]).wait()

    def weights_1(m):
        take(wa_r, m)
        for axis in range(2):
            pass_on(m, mine, axis, wb_s.at[m, axis], wb_r.at[m, axis])
        share(m, mine, 0)

    def weights_2(m):
        take(wb_r, m, 1 - m)
        pass_on(m, (at_z, at_y)[m], m, wc_s.at[m], wc_r.at[m])
        share(m, (at_z, at_y)[m], 2)
        take(wb_r, m, m)
        share(m, (at_y, at_z)[m], 1)

    def weights_3(m):
        take(wc_r, m)
        share(m, at_d, 3)

    def weights_4(m):
        pltpu.make_async_copy(wts.at[c, m], wts.at[c, m], own_r.at[m]).wait()
        for stage in range(4):
            take(wd_r, stage, m)

    fsend[...] = jnp.zeros_like(fsend)
    n3[...] = jnp.zeros_like(n3)
    tall[...] = jnp.zeros_like(tall)
    small[...] = jnp.zeros_like(small)
    for fetch in fetches:
        fetch.wait()
    small[0:2, 0:192] = gains[...].astype(F32)
    small[2:5, 0:192] = biases[...].astype(F32)
    small[5:6, :] = upb[...].astype(F32).reshape(1, D)
    for w_ref, b_ref, src, bsrc in ((w1, b1, fin, finb), (w2, b2, fout, foutb)):
        w_ref[...] = jnp.zeros_like(w_ref)
        b_ref[...] = jnp.zeros_like(b_ref)
        for at, re, im in zip((0, 256), parts(src[0, blk]), parts(src[1, blk])):
            w_ref[at:at + BS, 0:BS] = re
            w_ref[at:at + BS, 128:128 + BS] = im
            w_ref[at + 128:at + 128 + BS, 0:BS] = -im
            w_ref[at + 128:at + 128 + BS, 128:128 + BS] = re
        w_ref[512:768, :] = w_ref[0:256, :]
        b_ref[:, 0:BS] = bsrc[0, pl.ds(blk, 1), :]
        b_ref[:, 128:128 + BS] = bsrc[1, pl.ds(blk, 1), :]


    lane = lax.broadcasted_iota(jnp.int32, (W, 128), 1)
    for r in range(OWN):
        v = state[r]
        total = jnp.sum(v, -1, keepdims=True)
        squares = jnp.sum(v * v, -1, keepdims=True)
        tall[r * R:r * R + W, :] = jnp.where(lane == 0, total, jnp.where(lane == 1, squares, 0.0))
    stat[...] = tall[...].T[0:8, :]

    @pl.when(owner)
    def _():
        for m in range(2):
            pltpu.make_async_copy(shards[m], wts.at[c, m], own_r.at[m]).start()

    pl.semaphore_wait(barrier, ND - 1)
    for j in range(NC):
        @pl.when(c != j)
        def _(j=j):
            pltpu.make_async_remote_copy(
                stat, stats.at[c], st_s.at[j], st_r.at[c], device_id=(l, j), device_id_type=MESH).start()

        @pl.when(c == j)
        def _(j=j):
            pltpu.make_async_copy(stat, stats.at[j], st_r.at[j]).start()

    weights_0(0)
    for j in range(NC):
        pltpu.make_async_copy(stats.at[j], stats.at[j], st_r.at[j]).wait()
    sent_weights(0)
    weights_0(1)
    total = (stats[0] + stats[1]) + (stats[2] + stats[3])
    mean = total[0:1] / D
    spread = lax.rsqrt(total[1:2] / D - mean * mean + EPS)
    line = lax.broadcasted_iota(jnp.int32, (128, 640), 0)
    tall[...] = jnp.where(line == 0, mean, jnp.where(line == 1, spread, 0.0)).T
    for r in range(OWN):
        at = slice(r * R, r * R + W)
        n = (state[r] - tall[at, 0:1]) * tall[at, 1:2] * small[0:1, 0:192] + small[2:3, 0:192]
        hi, lo = parts(n)
        n3[0:W, 0:192] = hi
        n3[R:R + W, 0:192] = hi
        n3[2 * R:2 * R + W, 0:192] = lo
        lon = jnp.dot(fwd[...], n3[:, 0:192], preferred_element_type=F32)
        for j in range(2):
            fsend[2 * r + j, :, :, 0:BS] = lon[:, j * BS:(j + 1) * BS].reshape(G, 8, BS).astype(BF)

    for dx, dy, dz, dk in OTHERS:
        if dx:
            continue
        for r in range(OWN):
            pltpu.make_async_remote_copy(
                fsend.at[2 * r + cores[dk], groups[dz][dy]], frecv.at[l * OWN + r], f_s, f_r,
                device_id=(groups[dz][dy] * 2 + cores[dk], c), device_id_type=MESH).start()
    for r in range(OWN):
        pltpu.make_async_copy(fsend.at[2 * r + blk, l // 2], frecv.at[l * OWN + r], f_r).start()
    pl.when(owner)(lambda: weights_1(0))

    def send_state():
        for i in range(OWN):
            @pl.when(c != i)
            def _(i=i):
                a, b = to_owner(i)
                a.start()
                b.start()

            @pl.when(c == i)
            def _(i=i):
                pltpu.make_async_copy(state.at[i], xin.at[i], in_r.at[i]).start()
                pltpu.make_async_copy(small, smalls.at[i], sm_r.at[i]).start()

    def own_row():
        for j in range(NC):
            pltpu.make_async_copy(xin.at[j], xin.at[j], in_r.at[j]).wait()
            pltpu.make_async_copy(smalls.at[j], smalls.at[j], sm_r.at[j]).wait()
        par[0:5, :] = jnp.concatenate([smalls[j, 0:5, 0:192] for j in range(NC)], axis=1)
        v = jnp.concatenate([xin[j] for j in range(NC)], axis=1)
        x[0:W, :] = v + norm(v, par[0:1, :], par[2:3, :])
        x[W:R, :] = jnp.zeros((R - W, D), F32)

    def send_row():
        v = x[...]
        n = norm(v, par[0:1, :], par[2:3, :])
        x[...] = v + n
        hi, lo = parts(n)
        n3[0:R, :] = hi
        n3[R:2 * R, :] = hi
        n3[2 * R:3 * R, :] = lo
        lon = jnp.dot(fwd[...], n3[...], preferred_element_type=F32)
        for b in range(NB):
            fsend[b, :, :, 0:BS] = lon[:, b * BS:(b + 1) * BS].reshape(G, 8, BS).astype(BF)

        for dx, dy, dz, dk in OTHERS:
            pltpu.make_async_remote_copy(
                fsend.at[2 * xs[dx] + cores[dk], groups[dz][dy]], frecv.at[row], f_s, f_r,
                device_id=(groups[dz][dy] * 2 + cores[dk], xs[dx]), device_id_type=MESH).start()
        pltpu.make_async_copy(
            fsend.at[2 * c + blk, l // 2], frecv.at[row], f_r).start()

    def step(s, carry):
        pltpu.make_async_copy(frecv, frecv, f_r).wait()
        g32[...] = frecv[...].reshape(H * 8, 128).astype(F32)
        got = jnp.concatenate(
            [jnp.concatenate([g32[pl.ds(4 * i + m, H, stride=8), :] for m in range(4)], axis=1) for i in range(2)],
            axis=0).astype(BF)
        got = jnp.concatenate([got, got], axis=0)
        spec = jnp.dot(t_to[...], got, preferred_element_type=F32) * SCALE
        spec = jnp.concatenate(
            [jnp.concatenate([spec[i * H:(i + 1) * H, m * 128:(m + 1) * 128] for i in range(2)], axis=1)
             for m in range(4)], axis=0)
        hi, lo = parts(spec)
        first = jnp.dot(jnp.concatenate([hi, hi, lo], axis=1), w1[...], preferred_element_type=F32) + b1[...]
        hi, lo = parts(jnp.maximum(first, 0.0))
        second = jnp.dot(jnp.concatenate([hi, hi, lo], axis=1), w2[...], preferred_element_type=F32) + b2[...]
        second = jnp.where(second > SHRINK, second - SHRINK,
                           jnp.where(second < -SHRINK, second + SHRINK, 0.0))
        second = jnp.concatenate(
            [jnp.concatenate([second[m * H:(m + 1) * H, i * 128:(i + 1) * 128] for m in range(4)], axis=1)
             for i in range(2)], axis=0)
        hi, lo = parts(second)
        rows = jnp.dot(t_fro[...], jnp.concatenate([hi, hi, lo], axis=0), preferred_element_type=F32)
        for i in range(2):
            for m in range(4):
                g32[pl.ds(4 * i + m, H, stride=8), :] = rows[i * H:(i + 1) * H, m * 128:(m + 1) * 128]
        bsend[...] = g32[...].reshape(H, 8, 128).astype(BF)

        for dx, dy, dz, dk in OTHERS:
            dl, dc = groups[dz][dy] * 2 + cores[dk], xs[dx]

            @pl.when(dc < OWN)
            def _(dl=dl, dc=dc):
                pltpu.make_async_remote_copy(
                    bsend.at[dl * OWN + dc], brecv.at[2 * c + blk, l // 2], b_s, b_r,
                    device_id=(dl, dc), device_id_type=MESH).start()

        @pl.when(owner)
        def _():
            pltpu.make_async_copy(bsend.at[row], brecv.at[2 * c + blk, l // 2], b_r).start()

            @pl.when(s == 0)
            def _():
                weights_1(1)
                sent_weights(1)
                send_state()
                weights_2(0)
                weights_2(1)
                weights_3(0)
                own_row()

            pltpu.make_async_copy(brecv, brecv, b_r).wait()

            packed = jnp.concatenate(
                [brecv[b].reshape(128, 128)[:, 0:BS].astype(F32) for b in range(NB)], axis=1).astype(BF)
            packed = jnp.concatenate([packed, packed], axis=0)
            v = x[...] + jnp.dot(back[...], packed, preferred_element_type=F32) * SCALE
            x[...] = v
            nb[...] = norm(v, par[1:2, :], par[3:4, :]).astype(BF)

            @pl.when(s == 0)
            def _():
                weights_4(0)

            for q in range(NC):
                for j in range(3):
                    cols = slice(j * 256, (j + 1) * 256)
                    weight = wts[q, 0, :, :, :, :, cols].reshape(D, 256)
                    pre = jnp.dot(nb[...], weight, preferred_element_type=F32) + smalls[q, 5:6, cols]
                    act = 0.5 * pre * (1.0 + lax.erf(pre * math.sqrt(0.5)))
                    hid[:, q * 768 + j * 256:q * 768 + (j + 1) * 256] = act.astype(BF)

            @pl.when(s == 0)
            def _():
                weights_3(1)
                weights_4(1)

            for j in range(3):
                cols = slice(j * 256, (j + 1) * 256)
                weight = wts[:, 1, :, :, :, :, cols].reshape(FF, 256)
                x[:, cols] = x[:, cols] + jnp.dot(hid[...], weight, preferred_element_type=F32) + par[4:5, cols]

            @pl.when(s < STEPS - 1)
            def _():
                sent_f(s)
                send_row()

            pltpu.make_async_copy(bsend.at[0:95], bsend.at[0:95], b_s).wait()

        @pl.when(jnp.logical_not(owner))
        def _():
            @pl.when(s == 0)
            def _():
                sent_weights(1)
                send_state()
                sent_f(s)

            pltpu.make_async_copy(bsend, bsend, b_s).wait()

        return carry

    def sent_f(s):
        @pl.when(s == 0)
        def _():
            pltpu.make_async_copy(bsend.at[0:93], bsend.at[0:93], f_s).wait()

        @pl.when(s > 0)
        def _():
            pltpu.make_async_copy(fsend.at[0:7], fsend.at[0:7], f_s).wait()
            pltpu.make_async_copy(fsend.at[7, 0:15], fsend.at[7, 0:15], f_s).wait()

    lax.fori_loop(0, STEPS, step, 0)

    @pl.when(owner)
    def _():
        sent_f(1)
        ref = wts.at[pl.ds(0, 3), 0]
        pltpu.make_async_copy(ref, ref, wd_s).wait()
        for m in range(2):
            for axis in range(2):
                take(wb_s, m, axis)
            take(wc_s, m)

    for i in range(OWN):
        @pl.when(c != i)
        def _(i=i):
            a, b = to_owner(i)
            a.wait_send()
            b.wait_send()

    for j in range(NC):
        @pl.when(c != j)
        def _(j=j):
            pltpu.make_async_copy(stat, stat, st_s.at[j]).wait()

    @pl.when(owner)
    def _():
        for j in range(NC):
            xin[j] = x[0:W, j * 192:(j + 1) * 192]
        for j in range(NC):
            @pl.when(c != j)
            def _(j=j):
                pltpu.make_async_remote_copy(
                    xin.at[j], out.at[c], o_s.at[j], o_r.at[c],
                    device_id=(l, j), device_id_type=MESH).start()

        pltpu.make_async_copy(xin.at[c], out.at[c], o_r.at[c]).start()

    for i in range(OWN):
        pltpu.make_async_copy(out.at[i], out.at[i], o_r.at[i]).wait()

    @pl.when(owner)
    def _():
        for j in range(NC):
            @pl.when(c != j)
            def _(j=j):
                pltpu.make_async_copy(xin.at[0], xin.at[0], o_s.at[j]).wait()


def local(
    state, norm_gains, channel_biases, filter_in, filter_in_bias, filter_out, filter_out_bias,
    up_weight, up_bias, down_weight,
):
    up = up_weight.reshape(2, 4, 2, 48, 768)
    down = down_weight.reshape(2, 4, 2, 48, 768)
    fwd, back, t_to, t_fro = tables()
    vm = pl.BlockSpec(memory_space=pltpu.VMEM)
    hbm = pl.BlockSpec(memory_space=pltpu.HBM)
    sem = pltpu.SemaphoreType.DMA
    result = pl.pallas_call(
        kernel,
        out_shape=jax.ShapeDtypeStruct((OWN, W, 192), F32),
        in_specs=[hbm] * 14,
        out_specs=vm,
        scratch_shapes=[
            pltpu.VMEM((OWN, W, 192), F32),
            pltpu.VMEM((2, 192), BF),
            pltpu.VMEM((3, 192), BF),
            pltpu.VMEM((2, 2, BS, BS), F32),
            pltpu.VMEM((2, 2, BS), F32),
            pltpu.VMEM((2, 2, BS, BS), F32),
            pltpu.VMEM((2, 2, BS), F32),
            pltpu.VMEM((D,), BF),
            pltpu.VMEM((128, 3 * R), BF),
            pltpu.VMEM((R, 256), BF),
            pltpu.VMEM((192, 384), BF),
            pltpu.VMEM((192, 576), BF),
            pltpu.VMEM((8, D), F32),
            sem((12,)),
            pltpu.VMEM((NC, W, 192), F32),
            pltpu.VMEM((NC, 8, D), F32),
            pltpu.VMEM((R, D), F32),
            pltpu.VMEM((R, D), BF),
            pltpu.VMEM((NB, G, 8, 128), BF),
            pltpu.VMEM((H, 8, 128), BF),
            pltpu.VMEM((H, 8, 128), BF),
            pltpu.VMEM((NB, G, 8, 128), BF),
            pltpu.VMEM((768, 256), BF),
            pltpu.VMEM((1, 256), F32),
            pltpu.VMEM((768, 256), BF),
            pltpu.VMEM((1, 256), F32),
            pltpu.VMEM((8, D), F32),
            pltpu.VMEM((R, FF), BF),
            pltpu.VMEM((768, 128), F32),
            pltpu.VMEM((3 * R, D), BF),
            pltpu.VMEM((NC, 2, 2, 4, 2, 48, 768), BF),
            pltpu.VMEM((640, 128), F32),
            pltpu.VMEM((8, 640), F32),
            pltpu.VMEM((NC, 8, 640), F32),
            sem((OWN,)), sem((NC,)), sem((OWN,)), sem((NC,)),
            sem, sem, sem, sem, sem((NC,)), sem((OWN,)),
            sem((2,)), sem((2, OWN)), sem((2,)), sem((2, 2)), sem((2, 2)), sem((2,)), sem((2,)), sem, sem((4, 2)), sem((NC,)), sem((NC,)),
        ],
        compiler_params=pltpu.CompilerParams(
            collective_id=0, has_side_effects=True, vmem_limit_bytes=64 * 1024 * 1024 - 65536),
        name="rollout",
    )(
        state[0], norm_gains, channel_biases, filter_in, filter_in_bias, filter_out, filter_out_bias,
        up, up_bias, down, jnp.asarray(fwd), jnp.asarray(back), jnp.asarray(t_to), jnp.asarray(t_fro),
    )
    return result[None]


def solution(mesh):
    placed = (
        P(None, "lat", None, "ch"),
        P(None, "ch"),
        P(None, "ch"),
        P(None, "ch", None, None),
        P(None, "ch", None),
        P(None, "ch", None, None),
        P(None, "ch", None),
        P(None, "ch"),
        P("ch"),
        P("ch", None),
    )
    return jax.shard_map(
        local, mesh=mesh, in_specs=placed, out_specs=P(None, "lat", None, "ch"), check_vma=False
    )
```

time: 142 us -> 115 us (0.81)
  Pallas kernels: 134 us -> 111 us
  local copies, waits for them, and re-layouts: 6.29 us -> 4.31 us
    pallas_call x1, Pallas kernels: 134 us -> 111 us  [local(): pl.pallas_call(kernel, out_shape=jax.ShapeDtypeStruct((OWN, W, 192), F32)...]
    unnamed x19 -> x1, local copies, waits for them, and re-layouts: 3.75 us -> 1.89 us
where the time goes in v4:
time: 115 us
  Pallas kernels  111 us (97%)
  local copies, waits for them, and re-layouts  4.31 us (4%)
    pallas_call x1, Pallas kernels, local(): pl.pallas_call(kernel, out_shape=jax.ShapeDtypeStruct((OWN, W, 192), F32)...  111 us
    broadcast_in_dim x1, local copies, waits for them, and re-layouts, local(): return result[None]  2.43 us

profile of v4, /device:TPU:4, one launch (start us, length us, event | category | flops | bytes accessed | tf_op | source)
XLA Modules:
  0.0 115.0 jit_solution(7696994684460865260)
XLA Ops:
  0.0 1.9 %copy.18 = f32[1,3,180,192]{3,2,0,1:T(8,128)} copy(f32[1,3,180,192]{3,0,2,1:T(1,128)} %param.14) | data formatting | bytes 829440
  1.9 110.7 %rollout.1 = f32[3,180,192]{2,1,0:T(8,128)} custom-call(f32[3,180,192]{2,1,0:T(8,128)} %bitcast.7, bf16[2,192]{1,0:T(2,128)(2,1)} %gains_h.1, bf16[3,192]{1,0:T(4,128)(2,1)} %biases_h.1, f32[2,2,96,96]{3,2,1,0:T(8,128)} %fin_h.1, f32[2,2,96]{2,1,0:T(2,128)} %finb_h.1, f32[2,2,96,96]{3,2,1,0:T(8,128)} %fout_h.1, f32[2,2,96]{2,1,0:T(2,128)} %foutb_h.1, ...), custom_call_target="tpu_custom_call" | custom-call | tf_op jit(solution)/shard_map/rollout/pallas_call | solution.py:479
  112.6 2.4 %copy.15 = f32[1,3,180,192]{3,0,2,1:T(1,128)} copy(f32[1,3,180,192]{3,2,1,0:T(8,128)} %bitcast.6) | data formatting | bytes 829440 | tf_op jit(solution)/shard_map/broadcast_in_dim | solution.py:530

commit v5 on v4

--- a/solution.py
+++ b/solution.py
@@ -82,8 +82,8 @@
 def kernel(
     state_h, gains_h, biases_h, fin_h, finb_h, fout_h, foutb_h, up, upb_h, down, fwd_h, back_h, to_h, fro_h,
     out,
-    state, gains, biases, fin, finb, fout, foutb, upb, fwd, back, t_to, t_fro, small, h_s,
-    xin, smalls, x, nb, fsend, frecv, bsend, brecv, w1, b1, w2, b2, par, hid, g32, n3, wts, tall, stat, stats,
+    lines, state, gains, biases, fin, finb, fout, foutb, upb, fwd, back, t_to, t_fro, small, h_s,
+    xin, ends, smalls, x, nb, fsend, frecv, bsend, brecv, w1, b1, w2, b2, par, hid, g32, n3, wts, tall, stat, stats,
     in_s, in_r, sm_s, sm_r, f_s, f_r, b_s, b_r, o_s, o_r,
     own_r, wa_s, wa_r, wb_s, wb_r, wc_s, wc_r, wd_s, wd_r, st_s, st_r,
 ):
@@ -105,7 +105,7 @@
         pltpu.make_async_copy(src, dst, h_s.at[i])
         for i, (src, dst) in enumerate((
             (to_h, t_to), (fro_h, t_fro), (fin_h, fin), (fout_h, fout), (finb_h, finb), (foutb_h, foutb),
-            (gains_h, gains), (biases_h, biases), (upb_h, upb), (fwd_h, fwd), (back_h, back), (state_h, state)))
+            (gains_h, gains), (biases_h, biases), (upb_h, upb), (fwd_h, fwd), (back_h, back), (state_h, lines)))
     ]
     for fetch in fetches:
         fetch.start()
@@ -133,61 +133,69 @@
     def foreign(j):
         return lax.rem(c + 1 + j, NC)
 
-    three = wts.at[0, 0, 0, pl.ds(0, 3)]
+    three = wts.at[0, 0, 0, pl.ds(0, 3), 0]
 
     def take(sems, *at):
-        pltpu.make_async_copy(three, three, sems.at[at]).wait()
-
-    def pass_on(m, piece, axis, s_sem, r_sem):
+        pltpu.make_async_copy(three, three, sems.at[at] if at else sems).wait()
+
+    def pass_on(t, piece, axis, s_sem, r_sem):
         for j in range(3):
             for half, sign in ((0, 1), (1, 3)):
-                ref = wts.at[foreign(j), m, k, piece, half]
+                ref = wts.at[foreign(j), t // 2, k, piece, t % 2, :, pl.ds(half * 384, 384)]
                 to = groups[(0, sign)[axis]][(sign, 0)[axis]] * 2 + k
                 pltpu.make_async_remote_copy(
                     ref, ref, s_sem, r_sem, device_id=(to, c), device_id_type=MESH).start()
 
-    def share(m, piece, stage):
+    def share(t, piece, stage):
         for j in range(3):
-            ref = wts.at[foreign(j), m, k, piece]
+            ref = wts.at[foreign(j), t // 2, k, piece, t % 2]
             pltpu.make_async_remote_copy(
-                ref, ref, wd_s, wd_r.at[stage, m], device_id=(groups[0][0] * 2 + 1 - k, c), device_id_type=MESH).start()
-
-    def weights_0(m):
+                ref, ref, wd_s, wd_r.at[t, stage], device_id=(groups[0][0] * 2 + 1 - k, c),
+                device_id_type=MESH).start()
+
+    @pl.when(owner)
+    def _():
+        for m in range(2):
+            pltpu.make_async_copy(shards[m], wts.at[c, m], own_r.at[m]).start()
+
+    def weights_0(t):
         for i in range(OWN):
             @pl.when(c != i)
             def _(i=i):
                 pltpu.make_async_remote_copy(
-                    shards[m].at[k, mine], wts.at[c, m, k, mine], wa_s.at[m, i], wa_r.at[m],
-                    device_id=(l, i), device_id_type=MESH).start()
-
-    def sent_weights(m):
+                    shards[t // 2].at[k, mine, t % 2], wts.at[c, t // 2, k, mine, t % 2],
+                    wa_s.at[t, i], wa_r.at[t], device_id=(l, i), device_id_type=MESH).start()
+
+    def sent_weights(t):
         for i in range(OWN):
             @pl.when(c != i)
             def _(i=i):
-                ref = shards[m].at[k, mine]
-                pltpu.make_async_copy(ref, ref, wa_s.at[m, i]).wait()
-
-    def weights_1(m):
-        take(wa_r, m)
+                ref = shards[t // 2].at[k, mine, t % 2]
+                pltpu.make_async_copy(ref, ref, wa_s.at[t, i]).wait()
+
+    def weights_1(t):
+        take(wa_r, t)
         for axis in range(2):
-            pass_on(m, mine, axis, wb_s.at[m, axis], wb_r.at[m, axis])
-        share(m, mine, 0)
-
-    def weights_2(m):
-        take(wb_r, m, 1 - m)
-        pass_on(m, (at_z, at_y)[m], m, wc_s.at[m], wc_r.at[m])
-        share(m, (at_z, at_y)[m], 2)
-        take(wb_r, m, m)
-        share(m, (at_y, at_z)[m], 1)
-
-    def weights_3(m):
-        take(wc_r, m)
-        share(m, at_d, 3)
+            pass_on(t, mine, axis, wb_s.at[t, axis], wb_r.at[t, axis])
+        share(t, mine, 0)
+
+    def weights_2(t):
+        u = t % 2
+        take(wb_r, t, 1 - u)
+        pass_on(t, (at_z, at_y)[u], u, wc_s.at[t], wc_r.at[t])
+        share(t, (at_z, at_y)[u], 2)
+        take(wb_r, t, u)
+        share(t, (at_y, at_z)[u], 1)
+
+    def weights_3(t):
+        take(wc_r, t)
+        share(t, at_d, 3)
 
     def weights_4(m):
         pltpu.make_async_copy(wts.at[c, m], wts.at[c, m], own_r.at[m]).wait()
-        for stage in range(4):
-            take(wd_r, stage, m)
+        for t in (2 * m, 2 * m + 1):
+            for stage in range(4):
+                take(wd_r, t, stage)
 
     fsend[...] = jnp.zeros_like(fsend)
     n3[...] = jnp.zeros_like(n3)
@@ -195,6 +203,7 @@
     small[...] = jnp.zeros_like(small)
     for fetch in fetches:
         fetch.wait()
+    state[...] = lines[...].reshape(OWN, W, 192)
     small[0:2, 0:192] = gains[...].astype(F32)
     small[2:5, 0:192] = biases[...].astype(F32)
     small[5:6, :] = upb[...].astype(F32).reshape(1, D)
@@ -219,11 +228,6 @@
         tall[r * R:r * R + W, :] = jnp.where(lane == 0, total, jnp.where(lane == 1, squares, 0.0))
     stat[...] = tall[...].T[0:8, :]
 
-    @pl.when(owner)
-    def _():
-        for m in range(2):
-            pltpu.make_async_copy(shards[m], wts.at[c, m], own_r.at[m]).start()
-
     pl.semaphore_wait(barrier, ND - 1)
     for j in range(NC):
         @pl.when(c != j)
@@ -238,7 +242,6 @@
     weights_0(0)
     for j in range(NC):
         pltpu.make_async_copy(stats.at[j], stats.at[j], st_r.at[j]).wait()
-    sent_weights(0)
     weights_0(1)
     total = (stats[0] + stats[1]) + (stats[2] + stats[3])
     mean = total[0:1] / D
@@ -265,7 +268,11 @@
                 device_id=(groups[dz][dy] * 2 + cores[dk], c), device_id_type=MESH).start()
     for r in range(OWN):
         pltpu.make_async_copy(fsend.at[2 * r + blk, l // 2], frecv.at[l * OWN + r], f_r).start()
+    sent_weights(0)
     pl.when(owner)(lambda: weights_1(0))
+    sent_weights(1)
+    weights_0(2)
+    pl.when(owner)(lambda: weights_1(1))
 
     def send_state():
         for i in range(OWN):
@@ -310,6 +317,18 @@
 
     def step(s, carry):
         pltpu.make_async_copy(frecv, frecv, f_r).wait()
+
+        @pl.when(s == 0)
+        def _():
+            sent_weights(2)
+            weights_0(3)
+
+            @pl.when(owner)
+            def _():
+                weights_2(0)
+                weights_1(2)
+
+
         g32[...] = frecv[...].reshape(H * 8, 128).astype(F32)
         got = jnp.concatenate(
             [jnp.concatenate([g32[pl.ds(4 * i + m, H, stride=8), :] for m in range(4)], axis=1) for i in range(2)],
@@ -350,13 +369,16 @@
 
             @pl.when(s == 0)
             def _():
-                weights_1(1)
-                sent_weights(1)
+                weights_2(1)
+                weights_1(3)
+                sent_weights(3)
                 send_state()
-                weights_2(0)
-                weights_2(1)
+                weights_2(2)
                 weights_3(0)
+                weights_3(1)
+                weights_2(3)
                 own_row()
+                weights_3(2)
 
             pltpu.make_async_copy(brecv, brecv, b_r).wait()
 
@@ -369,6 +391,7 @@
 
             @pl.when(s == 0)
             def _():
+                weights_3(3)
                 weights_4(0)
 
             for q in range(NC):
@@ -381,7 +404,6 @@
 
             @pl.when(s == 0)
             def _():
-                weights_3(1)
                 weights_4(1)
 
             for j in range(3):
@@ -400,7 +422,7 @@
         def _():
             @pl.when(s == 0)
             def _():
-                sent_weights(1)
+                sent_weights(3)
                 send_state()
                 sent_f(s)
 
@@ -425,10 +447,10 @@
         sent_f(1)
         ref = wts.at[pl.ds(0, 3), 0]
         pltpu.make_async_copy(ref, ref, wd_s).wait()
-        for m in range(2):
+        for t in range(4):
             for axis in range(2):
-                take(wb_s, m, axis)
-            take(wc_s, m)
+                take(wb_s, t, axis)
+            take(wc_s, t)
 
     for i in range(OWN):
         @pl.when(c != i)
@@ -450,13 +472,14 @@
             @pl.when(c != j)
             def _(j=j):
                 pltpu.make_async_remote_copy(
-                    xin.at[j], out.at[c], o_s.at[j], o_r.at[c],
+                    xin.at[j], ends.at[c], o_s.at[j], o_r.at[c],
                     device_id=(l, j), device_id_type=MESH).start()
 
-        pltpu.make_async_copy(xin.at[c], out.at[c], o_r.at[c]).start()
+        pltpu.make_async_copy(xin.at[c], ends.at[c], o_r.at[c]).start()
 
     for i in range(OWN):
-        pltpu.make_async_copy(out.at[i], out.at[i], o_r.at[i]).wait()
+        pltpu.make_async_copy(ends.at[i], ends.at[i], o_r.at[i]).wait()
+        out[i] = ends[i].reshape(W, 1, 192)
 
     @pl.when(owner)
     def _():
@@ -478,10 +501,11 @@
     sem = pltpu.SemaphoreType.DMA
     result = pl.pallas_call(
         kernel,
-        out_shape=jax.ShapeDtypeStruct((OWN, W, 192), F32),
+        out_shape=jax.ShapeDtypeStruct((OWN, W, 1, 192), F32),
         in_specs=[hbm] * 14,
         out_specs=vm,
         scratch_shapes=[
+            pltpu.VMEM((OWN, W, 1, 192), F32),
             pltpu.VMEM((OWN, W, 192), F32),
             pltpu.VMEM((2, 192), BF),
             pltpu.VMEM((3, 192), BF),
@@ -497,6 +521,7 @@
             pltpu.VMEM((8, D), F32),
             sem((12,)),
             pltpu.VMEM((NC, W, 192), F32),
+            pltpu.VMEM((OWN, W, 192), F32),
             pltpu.VMEM((NC, 8, D), F32),
             pltpu.VMEM((R, D), F32),
             pltpu.VMEM((R, D), BF),
@@ -518,16 +543,16 @@
             pltpu.VMEM((NC, 8, 640), F32),
             sem((OWN,)), sem((NC,)), sem((OWN,)), sem((NC,)),
             sem, sem, sem, sem, sem((NC,)), sem((OWN,)),
-            sem((2,)), sem((2, OWN)), sem((2,)), sem((2, 2)), sem((2, 2)), sem((2,)), sem((2,)), sem, sem((4, 2)), sem((NC,)), sem((NC,)),
+            sem((2,)), sem((4, OWN)), sem((4,)), sem((4, 2)), sem((4, 2)), sem((4,)), sem((4,)), sem, sem((4, 4)), sem((NC,)), sem((NC,)),
         ],
         compiler_params=pltpu.CompilerParams(
-            collective_id=0, has_side_effects=True, vmem_limit_bytes=64 * 1024 * 1024 - 65536),
+            collective_id=0, has_side_effects=True, vmem_limit_bytes=62 * 1024 * 1024),
         name="rollout",
     )(
-        state[0], norm_gains, channel_biases, filter_in, filter_in_bias, filter_out, filter_out_bias,
+        state.reshape(OWN, W, 1, 192), norm_gains, channel_biases, filter_in, filter_in_bias, filter_out, filter_out_bias,
         up, up_bias, down, jnp.asarray(fwd), jnp.asarray(back), jnp.asarray(t_to), jnp.asarray(t_fro),
     )
-    return result[None]
+    return result.reshape(1, OWN, W, 192)
 
 
 def solution(mesh):

time: 115 us -> 111 us (0.965)
  Pallas kernels: 111 us -> 108 us
  local copies, waits for them, and re-layouts: 4.31 us -> 2.23 us
    broadcast_in_dim x1 -> x0, local copies, waits for them, and re-layouts: 2.43 us -> none  [local(): return result[None]]
    pallas_call x1, Pallas kernels: 111 us -> 108 us  [local(): pl.pallas_call(kernel, out_shape=jax.ShapeDtypeStruct((OWN, W, 1, 192), F...]
where the time goes in v5:
time: 111 us
  Pallas kernels  108 us (97%)
  local copies, waits for them, and re-layouts  2.23 us (2%)
    pallas_call x1, Pallas kernels, local(): pl.pallas_call(kernel, out_shape=jax.ShapeDtypeStruct((OWN, W, 1, 192), F...  108 us
    unnamed x1, local copies, waits for them, and re-layouts  2.23 us

profile of v5, /device:TPU:4, one launch (start us, length us, event | category | flops | bytes accessed | tf_op | source)
XLA Modules:
  0.0 110.5 jit_solution(162694860486213827)
XLA Ops:
  0.0 108.3 %rollout.1 = f32[3,180,1,192]{3,2,1,0:T(1,128)} custom-call(f32[3,180,1,192]{3,2,1,0:T(1,128)} %bitcast.7, bf16[2,192]{1,0:T(2,128)(2,1)} %gains_h.1, bf16[3,192]{1,0:T(4,128)(2,1)} %biases_h.1, f32[2,2,96,96]{3,2,1,0:T(8,128)} %fin_h.1, f32[2,2,96]{2,1,0:T(2,128)} %finb_h.1, f32[2,2,96,96]{3,2,1,0:T(8,128)} %fout_h.1, f32[2,2,96]{2,1,0:T(2,128)} %foutb_h.1, ...), custom_call_target="tpu_custom_call" | custom-call | tf_op jit(solution)/shard_map/rollout/pallas_call | solution.py:502
  108.3 2.2 %copy.16 = f32[1,3,180,192]{3,0,2,1:T(1,128)} copy(f32[1,3,180,192]{3,0,2,1:T(1,128)} %bitcast.4) | data formatting | bytes 829440

commit v6 on v5

--- a/solution.py
+++ b/solution.py
@@ -393,8 +393,9 @@
             def _():
                 weights_3(3)
                 weights_4(0)
-
-            for q in range(NC):
+                weights_4(1)
+
+            def up_part(q):
                 for j in range(3):
                     cols = slice(j * 256, (j + 1) * 256)
                     weight = wts[q, 0, :, :, :, :, cols].reshape(D, 256)
@@ -402,14 +403,20 @@
                     act = 0.5 * pre * (1.0 + lax.erf(pre * math.sqrt(0.5)))
                     hid[:, q * 768 + j * 256:q * 768 + (j + 1) * 256] = act.astype(BF)
 
-            @pl.when(s == 0)
-            def _():
-                weights_4(1)
-
-            for j in range(3):
-                cols = slice(j * 256, (j + 1) * 256)
-                weight = wts[:, 1, :, :, :, :, cols].reshape(FF, 256)
-                x[:, cols] = x[:, cols] + jnp.dot(hid[...], weight, preferred_element_type=F32) + par[4:5, cols]
+            def down_part(q):
+                for j in range(3):
+                    cols = slice(j * 256, (j + 1) * 256)
+                    weight = wts[q, 1, :, :, :, :, cols].reshape(D, 256)
+                    mixed = jnp.dot(hid[:, q * 768:(q + 1) * 768], weight, preferred_element_type=F32)
+                    if q == 0:
+                        mixed = mixed + par[4:5, cols]
+                    x[:, cols] = x[:, cols] + mixed
+
+            up_part(0)
+            for q in range(1, NC):
+                up_part(q)
+                down_part(q - 1)
+            down_part(NC - 1)
 
             @pl.when(s < STEPS - 1)
             def _():

time: 111 us -> 109 us (0.982)
    pallas_call x1, Pallas kernels: 108 us -> 107 us  [local(): pl.pallas_call(kernel, out_shape=jax.ShapeDtypeStruct((OWN, W, 1, 192), F...]
where the time goes in v6:
time: 109 us
  Pallas kernels  107 us (98%)
  local copies, waits for them, and re-layouts  2.23 us (2%)
    pallas_call x1, Pallas kernels, local(): pl.pallas_call(kernel, out_shape=jax.ShapeDtypeStruct((OWN, W, 1, 192), F...  107 us
    unnamed x1, local copies, waits for them, and re-layouts  2.23 us

profile of v6, /device:TPU:4, one launch (start us, length us, event | category | flops | bytes accessed | tf_op | source)
XLA Modules:
  0.0 109.0 jit_solution(5674232112764821174)
XLA Ops:
  0.0 106.8 %rollout.1 = f32[3,180,1,192]{3,2,1,0:T(1,128)} custom-call(f32[3,180,1,192]{3,2,1,0:T(1,128)} %bitcast.7, bf16[2,192]{1,0:T(2,128)(2,1)} %gains_h.1, bf16[3,192]{1,0:T(4,128)(2,1)} %biases_h.1, f32[2,2,96,96]{3,2,1,0:T(8,128)} %fin_h.1, f32[2,2,96]{2,1,0:T(2,128)} %finb_h.1, f32[2,2,96,96]{3,2,1,0:T(8,128)} %fout_h.1, f32[2,2,96]{2,1,0:T(2,128)} %foutb_h.1, ...), custom_call_target="tpu_custom_call" | custom-call | tf_op jit(solution)/shard_map/rollout/pallas_call | solution.py:509
  106.8 2.2 %copy.16 = f32[1,3,180,192]{3,0,2,1:T(1,128)} copy(f32[1,3,180,192]{3,0,2,1:T(1,128)} %bitcast.4) | data formatting | bytes 829440

commit v7 on v6

--- a/solution.py
+++ b/solution.py
@@ -83,9 +83,9 @@
     state_h, gains_h, biases_h, fin_h, finb_h, fout_h, foutb_h, up, upb_h, down, fwd_h, back_h, to_h, fro_h,
     out,
     lines, state, gains, biases, fin, finb, fout, foutb, upb, fwd, back, t_to, t_fro, small, h_s,
-    xin, ends, smalls, x, nb, fsend, frecv, bsend, brecv, w1, b1, w2, b2, par, hid, g32, n3, wts, tall, stat, stats,
+    xin, early, late, earlies, lates, smalls, x, nb, fsend, frecv, bsend, brecv, w1, b1, w2, b2, par, hid, g32, n3, wts, tall, stat, stats,
     in_s, in_r, sm_s, sm_r, f_s, f_r, b_s, b_r, o_s, o_r,
-    own_r, wa_s, wa_r, wb_s, wb_r, wc_s, wc_r, wd_s, wd_r, st_s, st_r,
+    own_r, wa_s, wa_r, wb_s, wb_r, wc_s, wc_r, wd_s, wd_r, st_s, st_r, e_s, e_r,
 ):
     l = lax.axis_index("lat")
     c = lax.axis_index("ch")
@@ -273,6 +273,18 @@
     sent_weights(1)
     weights_0(2)
     pl.when(owner)(lambda: weights_1(1))
+
+    def hand_out(src, dst, s_sems, r_sems):
+        for j in range(NC):
+            src[j] = (x[0:W, j * 192:(j + 1) * 192] - xin[j]).astype(BF)
+        for j in range(NC):
+            @pl.when(c != j)
+            def _(j=j):
+                pltpu.make_async_remote_copy(
+                    src.at[j], dst.at[c], s_sems.at[j], r_sems.at[c],
+                    device_id=(l, j), device_id_type=MESH).start()
+
+        pltpu.make_async_copy(src.at[c], dst.at[c], r_sems.at[c]).start()
 
     def send_state():
         for i in range(OWN):
@@ -387,6 +399,12 @@
             packed = jnp.concatenate([packed, packed], axis=0)
             v = x[...] + jnp.dot(back[...], packed, preferred_element_type=F32) * SCALE
             x[...] = v
+            @pl.when(s == STEPS - 2)
+            def _():
+                hand_out(early, earlies, e_s, e_r)
+                for j in range(NC):
+                    xin[j] = xin[j] + early[j].astype(F32)
+
             nb[...] = norm(v, par[1:2, :], par[3:4, :]).astype(BF)
 
             @pl.when(s == 0)
@@ -473,27 +491,22 @@
 
     @pl.when(owner)
     def _():
-        for j in range(NC):
-            xin[j] = x[0:W, j * 192:(j + 1) * 192]
-        for j in range(NC):
-            @pl.when(c != j)
-            def _(j=j):
-                pltpu.make_async_remote_copy(
-                    xin.at[j], ends.at[c], o_s.at[j], o_r.at[c],
-                    device_id=(l, j), device_id_type=MESH).start()
-
-        pltpu.make_async_copy(xin.at[c], ends.at[c], o_r.at[c]).start()
+        hand_out(late, lates, o_s, o_r)
 
     for i in range(OWN):
-        pltpu.make_async_copy(ends.at[i], ends.at[i], o_r.at[i]).wait()
-        out[i] = ends[i].reshape(W, 1, 192)
+        pltpu.make_async_copy(earlies.at[i], earlies.at[i], e_r.at[i]).wait()
+        state[i] = state[i] + earlies[i].astype(F32)
+    for i in range(OWN):
+        pltpu.make_async_copy(lates.at[i], lates.at[i], o_r.at[i]).wait()
+        out[i] = (state[i] + lates[i].astype(F32)).reshape(W, 1, 192)
 
     @pl.when(owner)
     def _():
         for j in range(NC):
             @pl.when(c != j)
             def _(j=j):
-                pltpu.make_async_copy(xin.at[0], xin.at[0], o_s.at[j]).wait()
+                pltpu.make_async_copy(early.at[0], early.at[0], e_s.at[j]).wait()
+                pltpu.make_async_copy(late.at[0], late.at[0], o_s.at[j]).wait()
 
 
 def local(
@@ -528,7 +541,10 @@
             pltpu.VMEM((8, D), F32),
             sem((12,)),
             pltpu.VMEM((NC, W, 192), F32),
-            pltpu.VMEM((OWN, W, 192), F32),
+            pltpu.VMEM((NC, W, 192), BF),
+            pltpu.VMEM((NC, W, 192), BF),
+            pltpu.VMEM((OWN, W, 192), BF),
+            pltpu.VMEM((OWN, W, 192), BF),
             pltpu.VMEM((NC, 8, D), F32),
             pltpu.VMEM((R, D), F32),
             pltpu.VMEM((R, D), BF),
@@ -550,7 +566,7 @@
             pltpu.VMEM((NC, 8, 640), F32),
             sem((OWN,)), sem((NC,)), sem((OWN,)), sem((NC,)),
             sem, sem, sem, sem, sem((NC,)), sem((OWN,)),
-            sem((2,)), sem((4, OWN)), sem((4,)), sem((4, 2)), sem((4, 2)), sem((4,)), sem((4,)), sem, sem((4, 4)), sem((NC,)), sem((NC,)),
+            sem((2,)), sem((4, OWN)), sem((4,)), sem((4, 2)), sem((4, 2)), sem((4,)), sem((4,)), sem, sem((4, 4)), sem((NC,)), sem((NC,)), sem((NC,)), sem((OWN,)),
         ],
         compiler_params=pltpu.CompilerParams(
             collective_id=0, has_side_effects=True, vmem_limit_bytes=62 * 1024 * 1024),

time: 109 us -> 107 us (0.982)
  Pallas kernels: 107 us -> 105 us
    pallas_call x1, Pallas kernels: 107 us -> 105 us  [local(): pl.pallas_call(kernel, out_shape=jax.ShapeDtypeStruct((OWN, W, 1, 192), F...]
where the time goes in v7:
time: 107 us
  Pallas kernels  105 us (98%)
  local copies, waits for them, and re-layouts  2.23 us (2%)
    pallas_call x1, Pallas kernels, local(): pl.pallas_call(kernel, out_shape=jax.ShapeDtypeStruct((OWN, W, 1, 192), F...  105 us
    unnamed x1, local copies, waits for them, and re-layouts  2.23 us

profile of v7, /device:TPU:4, one launch (start us, length us, event | category | flops | bytes accessed | tf_op | source)
XLA Modules:
  0.0 106.8 jit_solution(4168535362210488343)
XLA Ops:
  0.0 104.5 %rollout.1 = f32[3,180,1,192]{3,2,1,0:T(1,128)} custom-call(f32[3,180,1,192]{3,2,1,0:T(1,128)} %bitcast.7, bf16[2,192]{1,0:T(2,128)(2,1)} %gains_h.1, bf16[3,192]{1,0:T(4,128)(2,1)} %biases_h.1, f32[2,2,96,96]{3,2,1,0:T(8,128)} %fin_h.1, f32[2,2,96]{2,1,0:T(2,128)} %finb_h.1, f32[2,2,96,96]{3,2,1,0:T(8,128)} %fout_h.1, f32[2,2,96]{2,1,0:T(2,128)} %foutb_h.1, ...), custom_call_target="tpu_custom_call" | custom-call | tf_op jit(solution)/shard_map/rollout/pallas_call | solution.py:522
  104.5 2.2 %copy.16 = f32[1,3,180,192]{3,0,2,1:T(1,128)} copy(f32[1,3,180,192]{3,0,2,1:T(1,128)} %bitcast.4) | data formatting | bytes 829440

commit v8 on v7

--- a/solution.py
+++ b/solution.py
@@ -399,7 +399,7 @@
             packed = jnp.concatenate([packed, packed], axis=0)
             v = x[...] + jnp.dot(back[...], packed, preferred_element_type=F32) * SCALE
             x[...] = v
-            @pl.when(s == STEPS - 2)
+            @pl.when(s == STEPS - 1)
             def _():
                 hand_out(early, earlies, e_s, e_r)
                 for j in range(NC):

time: 107 us -> 107 us (level)
  no operation moved by 1% of the time
where the time goes in v8:
time: 107 us
  Pallas kernels  105 us (98%)
  local copies, waits for them, and re-layouts  2.23 us (2%)
    pallas_call x1, Pallas kernels, local(): pl.pallas_call(kernel, out_shape=jax.ShapeDtypeStruct((OWN, W, 1, 192), F...  105 us
    unnamed x1, local copies, waits for them, and re-layouts  2.23 us

profile of v8, /device:TPU:4, one launch (start us, length us, event | category | flops | bytes accessed | tf_op | source)
XLA Modules:
  0.0 107.1 jit_solution(3586781481801480183)
XLA Ops:
  0.0 104.8 %rollout.1 = f32[3,180,1,192]{3,2,1,0:T(1,128)} custom-call(f32[3,180,1,192]{3,2,1,0:T(1,128)} %bitcast.7, bf16[2,192]{1,0:T(2,128)(2,1)} %gains_h.1, bf16[3,192]{1,0:T(4,128)(2,1)} %biases_h.1, f32[2,2,96,96]{3,2,1,0:T(8,128)} %fin_h.1, f32[2,2,96]{2,1,0:T(2,128)} %finb_h.1, f32[2,2,96,96]{3,2,1,0:T(8,128)} %fout_h.1, f32[2,2,96]{2,1,0:T(2,128)} %foutb_h.1, ...), custom_call_target="tpu_custom_call" | custom-call | tf_op jit(solution)/shard_map/rollout/pallas_call | solution.py:522
  104.8 2.2 %copy.16 = f32[1,3,180,192]{3,0,2,1:T(1,128)} copy(f32[1,3,180,192]{3,0,2,1:T(1,128)} %bitcast.4) | data formatting | bytes 829440

commit v9 on v8

--- a/solution.py
+++ b/solution.py
@@ -274,9 +274,10 @@
     weights_0(2)
     pl.when(owner)(lambda: weights_1(1))
 
-    def hand_out(src, dst, s_sems, r_sems):
+    def hand_out(src, dst, s_sems, r_sems, sent=None):
         for j in range(NC):
-            src[j] = (x[0:W, j * 192:(j + 1) * 192] - xin[j]).astype(BF)
+            have = xin[j] if sent is None else xin[j] + sent[j].astype(F32)
+            src[j] = (x[0:W, j * 192:(j + 1) * 192] - have).astype(BF)
         for j in range(NC):
             @pl.when(c != j)
             def _(j=j):
@@ -402,8 +403,6 @@
             @pl.when(s == STEPS - 1)
             def _():
                 hand_out(early, earlies, e_s, e_r)
-                for j in range(NC):
-                    xin[j] = xin[j] + early[j].astype(F32)
 
             nb[...] = norm(v, par[1:2, :], par[3:4, :]).astype(BF)
 
@@ -491,7 +490,7 @@
 
     @pl.when(owner)
     def _():
-        hand_out(late, lates, o_s, o_r)
+        hand_out(late, lates, o_s, o_r, early)
 
     for i in range(OWN):
         pltpu.make_async_copy(earlies.at[i], earlies.at[i], e_r.at[i]).wait()

time: 107 us -> 107 us (level)
  no operation moved by 1% of the time
where the time goes in v9:
time: 107 us
  Pallas kernels  105 us (98%)
  local copies, waits for them, and re-layouts  2.23 us (2%)
    pallas_call x1, Pallas kernels, local(): pl.pallas_call(kernel, out_shape=jax.ShapeDtypeStruct((OWN, W, 1, 192), F...  105 us
    unnamed x1, local copies, waits for them, and re-layouts  2.23 us

profile of v9, /device:TPU:4, one launch (start us, length us, event | category | flops | bytes accessed | tf_op | source)
XLA Modules:
  0.0 107.1 jit_solution(3037049087474467750)
XLA Ops:
  0.0 104.8 %rollout.1 = f32[3,180,1,192]{3,2,1,0:T(1,128)} custom-call(f32[3,180,1,192]{3,2,1,0:T(1,128)} %bitcast.7, bf16[2,192]{1,0:T(2,128)(2,1)} %gains_h.1, bf16[3,192]{1,0:T(4,128)(2,1)} %biases_h.1, f32[2,2,96,96]{3,2,1,0:T(8,128)} %fin_h.1, f32[2,2,96]{2,1,0:T(2,128)} %finb_h.1, f32[2,2,96,96]{3,2,1,0:T(8,128)} %fout_h.1, f32[2,2,96]{2,1,0:T(2,128)} %foutb_h.1, ...), custom_call_target="tpu_custom_call" | custom-call | tf_op jit(solution)/shard_map/rollout/pallas_call | solution.py:521
  104.8 2.2 %copy.16 = f32[1,3,180,192]{3,0,2,1:T(1,128)} copy(f32[1,3,180,192]{3,0,2,1:T(1,128)} %bitcast.4) | data formatting | bytes 829440
